TPU v7x, 16 devices: a 4x2x1 block of a 4x4x8 slice. The times are simulated.
16 devices in a mesh: rep: 2 (over y, z), dp: 8 (over x, core).
Axes of the slice: x: 4, y: 2, z: 1, core: 2. Of those that a mesh axis runs over, the one named last changes fastest.
The devices are a block of a 4x4x8 slice.
Arguments:
- x: bfloat16 [16, 2048, 640], P(('rep', 'dp')), parts along dimension 0
- dy: bfloat16 [16, 2048, 640], P(('rep', 'dp')), parts along dimension 0
- w_gate: bfloat16 [2, 640, 3456], replicated
- w_up: bfloat16 [2, 640, 3456], replicated
- w_down: bfloat16 [2, 3456, 640], replicated
- m_w_gate: float32 [2, 640, 3456], replicated
- m_w_up: float32 [2, 640, 3456], replicated
- m_w_down: float32 [2, 3456, 640], replicated
- v_w_gate: float32 [2, 640, 3456], replicated
- v_w_up: float32 [2, 640, 3456], replicated
- v_w_down: float32 [2, 3456, 640], replicated
Outputs:
- output 1: bfloat16 [4, 640, 3456], P('rep'), parts along dimension 0
- output 2: bfloat16 [4, 640, 3456], P('rep'), parts along dimension 0
- output 3: bfloat16 [4, 3456, 640], P('rep'), parts along dimension 0
- output 4: float32 [4, 640, 3456], P('rep'), parts along dimension 0
- output 5: float32 [4, 640, 3456], P('rep'), parts along dimension 0
- output 6: float32 [4, 3456, 640], P('rep'), parts along dimension 0
- output 7: float32 [4, 640, 3456], P('rep'), parts along dimension 0
- output 8: float32 [4, 640, 3456], P('rep'), parts along dimension 0
- output 9: float32 [4, 3456, 640], P('rep'), parts along dimension 0
There are 2 independent parts. A program takes and returns all parts, laid end to end along the dimension named above; an argument that names none is the same for every part.
All inputs are finite; a program needn't handle non-finite values.
Results may differ from a plain program's by a relative error of at most 0.022.
Values are sent between devices in bfloat16 or wider.
A program may use at most 768 MiB of HBM per device.

v0:
```python
import jax
import jax.numpy as jnp
from jax import lax
from jax.sharding import PartitionSpec as P

NAMES = ("w_gate", "w_up", "w_down")


def matmul(a, w):
    return jnp.dot(a, w, preferred_element_type=jnp.float32).astype(jnp.bfloat16)


def normed(h):
    wide = h.astype(jnp.float32)
    scale = lax.rsqrt(jnp.mean(wide**2, -1, keepdims=True) + 1e-6)
    return (wide * scale).astype(jnp.bfloat16)


def layer(h, w):
    a = normed(h)
    gate = jnp.dot(a, w["w_gate"], preferred_element_type=jnp.float32)
    up = jnp.dot(a, w["w_up"], preferred_element_type=jnp.float32)
    return h + matmul((jax.nn.silu(gate) * up).astype(jnp.bfloat16), w["w_down"])


def adamw(w, m, v, g):
    m = 0.9 * m + 0.1 * g
    v = 0.95 * v + 0.05 * g * g
    step = m * lax.rsqrt(v + 1e-8) + 0.1 * w
    return (w - 0.02 * step).astype(jnp.bfloat16), m, v


def clipped(gradients, sum_of_squares, count):
    factor = jnp.minimum(1.0, 0.5 * lax.rsqrt(sum_of_squares / count + 1e-30))
    return [g * factor for g in gradients]


def solution(mesh):
    def step(x, dy, *arrays):
        weights, m, v = (arrays[i : i + 3] for i in (0, 3, 6))
        layers = weights[0].shape[0]
        h, kept = x[0], []
        for number in range(layers):
            kept.append(h)
            h = layer(h, {name: w[number] for name, w in zip(NAMES, weights, strict=True)})
        by_h, summed = dy[0], [None] * layers
        for number in reversed(range(layers)):
            _, back = jax.vjp(lambda w, h: layer(h, w), {name: w[number] for name, w in zip(NAMES, weights, strict=True)}, kept[number])
            by_w, by_h = back(by_h)
            summed[number] = [lax.psum(by_w[name], "dp") for name in NAMES]
        gradients = [jnp.stack([summed[number][i] for number in range(layers)]).astype(jnp.float32) for i in range(3)]
        gradients = clipped(gradients, sum(jnp.sum(g * g) for g in gradients), sum(g.size for g in gradients))
        new = [adamw(w.astype(jnp.float32), m, v, g) for w, m, v, g in zip(weights, m, v, gradients, strict=True)]
        return tuple(one[which] for which in range(3) for one in new)

    return jax.shard_map(
        step,
        mesh=mesh,
        in_specs=(P(("rep", "dp"), None, None),) * 2 + (P(None, None, None),) * 9,
        out_specs=(P("rep", None, None),) * 9,
        check_vma=False,
    )
```

profile of v0, /device:TPU:113, one launch (start us, length us, event | category | flops | bytes accessed | tf_op | source)
XLA Modules:
  0.0 728.1 jit_solution(6974457710553593345)
XLA Ops:
  7.2 0.1 all-reduce.3.cloned.1.call-start
  7.3 3.0 copy.20
  10.3 0.0 copy-start.1
  10.3 0.6 fusion.50
  10.8 4.7 copy.21
  15.6 17.4 %convolution_convert_fusion.1 = bf16[2048,3456]{1,0:T(8,128)(2,1)} fusion(bf16[2,3456,640]{2,1,0:T(8,128)(2,1)} %param.15, bf16[1,2048,640]{2,1,0:T(8,128)(2,1)} %param.12), kind=kOutput, calls=%fused_computation.59 | convolution fusion | flops 9066774528 | bytes 21200896 | tf_op jit(solution)/shard_map/transpose(jvp())/dot_general | solution.py:10
  33.0 0.0 copy-done.6
  33.0 17.7 %fusion.71 = f32[2048,3456]{1,0:T(8,128)} fusion(bf16[2,640,3456]{2,1,0:T(8,128)(2,1)} %param.13, bf16[1,2048,640]{2,1,0:T(8,128)(2,1)S(1)} %copy-done.6, f32[2048]{0:T(1024)S(1)} %add_rsqrt_fusion), kind=kOutput, calls=%fused_computation.105 | convolution fusion | flops 9063628800 | bytes 35364864 | tf_op jit(solution)/shard_map/dot_general | solution.py:21
  50.6 0.0 copy-done.9
  50.7 30.1 %multiply_convert_fusion.1 = (bf16[2048,3456]{1,0:T(8,128)(2,1)}, f32[2048,3456]{1,0:T(8,128)}) fusion(f32[2048,3456]{1,0:T(8,128)} %fusion.71, bf16[2,640,3456]{2,1,0:T(8,128)(2,1)} %param.14, bf16[1,2048,640]{2,1,0:T(8,128)(2,1)} %param.11, f32[2048]{0:T(1024)S(1)} %add_rsqrt_fusion), kind=kOutput, calls=%fused_computation.17 | convolution fusion | flops 9106096128 | bytes 77832192 | tf_op jit(solution)/shard_map/dot_general | solution.py:22
  80.7 0.0 copy-done.1
  80.7 14.6 %fusion.54 = (f32[2048]{0:T(1024)S(1)}, bf16[2048,640]{0,1:T(8,128)(2,1)S(1)}) fusion(bf16[2048,3456]{1,0:T(8,128)(2,1)} %get-tuple-element.24, bf16[2,3456,640]{2,1,0:T(8,128)(2,1)} %param.15, bf16[1,2048,640]{1,2,0:T(8,128)(2,1)S(1)} %copy.20), kind=kOutput, calls=%fused_computation.88 | convolution fusion | flops 9066248192 | bytes 23830528 | tf_op jit(solution)/shard_map/dot_general | solution.py:10
  95.4 0.0 copy-start.7
  95.4 0.0 copy-start.3
  95.4 0.6 copy-done.7
  96.0 0.9 copy-done.3
  96.9 17.5 %fusion.58 = f32[2048,3456]{1,0:T(8,128)} fusion(bf16[2,640,3456]{2,1,0:T(8,128)(2,1)} %param.14, bf16[2048,640]{0,1:T(8,128)(2,1)S(1)} %get-tuple-element.27, f32[2048]{0:T(1024)S(1)} %fusion.109), kind=kOutput, calls=%fused_computation.92 | convolution fusion | flops 9063628800 | bytes 35364864 | tf_op jit(solution)/shard_map/jvp()/dot_general | solution.py:22
  114.4 39.0 %fusion.2 = (bf16[2048,3456]{1,0:T(8,128)(2,1)}, f32[2048,3456]{1,0:T(8,128)}) fusion(f32[2048,3456]{1,0:T(8,128)} %fusion.58, bf16[2048,3456]{1,0:T(8,128)(2,1)} %convolution_convert_fusion.1, bf16[2,640,3456]{2,1,0:T(8,128)(2,1)} %param.13, bf16[2048,640]{0,1:T(8,128)(2,1)} %copy-done.3, f32[2048]{0:T(1024)S(1)} %fusion.109), kind=kOutput, calls=%fused_computation.8 | convolution fusion | flops 9148563456 | bytes 91987968 | tf_op jit(solution)/shard_map/jvp()/dot_general | solution.py:21
  153.4 19.3 %fusion.88 = bf16[2048,640]{0,1:T(8,128)(2,1)} fusion(bf16[2,640,3456]{2,1,0:T(8,128)(2,1)} %param.14, bf16[2048,3456]{1,0:T(8,128)(2,1)} %convolution_convert_fusion.1, f32[2048,3456]{1,0:T(8,128)} %get-tuple-element.29), kind=kOutput, calls=%fused_computation.118 | convolution fusion | flops 9103474688 | bytes 49512448 | tf_op jit(solution)/shard_map/transpose(jvp())/dot_general | solution.py:22
  172.7 25.0 %fusion.46 = bf16[1,3456,640]{2,1,0:T(8,128)(2,1)} fusion(f32[2048,3456]{1,0:T(8,128)} %fusion.58, bf16[1,2048,640]{2,1,0:T(8,128)(2,1)} %param.12, f32[2048,3456]{1,0:T(8,128)} %get-tuple-element.29), kind=kOutput, calls=%fused_computation.80 | convolution fusion | flops 9104375808 | bytes 63668224 | tf_op jit(solution)/shard_map/transpose(jvp())/dot_general | solution.py:10
  197.7 0.0 copy-done.4
  197.8 15.0 %fusion.56 = (f32[2048]{0:T(1024)S(1)}, bf16[2048,640]{0,1:T(8,128)(2,1)S(1)}) fusion(bf16[2048,640]{0,1:T(8,128)(2,1)S(1)} %copy-done.4, bf16[2048,640]{0,1:T(8,128)(2,1)} %fusion.88, bf16[2048,3456]{1,0:T(8,128)(2,1)} %get-tuple-element.28, bf16[2,640,3456]{2,1,0:T(8,128)(2,1)} %param.13), kind=kOutput, calls=%fused_computation.90 | convolution fusion | flops 9066248192 | bytes 26451968 | tf_op jit(solution)/shard_map/transpose(jvp())/dot_general | solution.py:21
  212.7 0.0 copy-done.8
  212.8 0.0 copy-done
  212.8 0.0 slice-start.6
  212.8 1.8 fusion.98
  214.6 0.0 copy-start.5
  214.6 1.5 copy-done.5
  216.1 17.0 %fusion.47 = bf16[1,3456,640]{2,1,0:T(8,128)(2,1)} fusion(bf16[2048,3456]{1,0:T(8,128)(2,1)} %get-tuple-element.24, bf16[2048,640]{0,1:T(8,128)(2,1)S(1)} %fusion.98), kind=kOutput, calls=%fused_computation.81 | convolution fusion | flops 9061908480 | bytes 21200896 | tf_op jit(solution)/shard_map/transpose(jvp())/dot_general | solution.py:10
  233.1 0.0 slice-done.6
  233.1 0.0 slice-done.7
  233.2 16.7 %convolution_convert_fusion = bf16[2048,3456]{1,0:T(8,128)(2,1)} fusion(bf16[2048,640]{0,1:T(8,128)(2,1)} %copy-done.5, bf16[2,3456,640]{2,1,0:T(8,128)(2,1)S(1)} %bitcast.87), kind=kOutput, calls=%fused_computation.58 | convolution fusion | flops 9066774528 | bytes 21200896 | tf_op jit(solution)/shard_map/transpose(jvp())/dot_general | solution.py:10
  249.8 20.5 %fusion.49 = bf16[1,640,3456]{2,1,0:T(8,128)(2,1)} fusion(bf16[2048,3456]{1,0:T(8,128)(2,1)} %convolution_convert_fusion.1, bf16[2048,640]{0,1:T(8,128)(2,1)S(1)} %copy-done.4, f32[2048]{0:T(1024)S(1)} %fusion.109, f32[2048,3456]{1,0:T(8,128)} %get-tuple-element.29), kind=kOutput, calls=%fused_computation.83 | convolution fusion | flops 9108307968 | bytes 49520640 | tf_op jit(solution)/shard_map/transpose(jvp())/dot_general | solution.py:22
  270.4 14.4 %fusion.42 = bf16[1,640,3456]{2,1,0:T(8,128)(2,1)} fusion(bf16[2048,3456]{1,0:T(8,128)(2,1)} %get-tuple-element.28, bf16[2048,640]{0,1:T(8,128)(2,1)S(1)} %copy-done.4, f32[2048]{0:T(1024)S(1)} %fusion.109), kind=kOutput, calls=%fused_computation.78 | convolution fusion | flops 9063628800 | bytes 21209088 | tf_op jit(solution)/shard_map/transpose(jvp())/dot_general | solution.py:21
  284.8 0.0 copy-done.2
  284.8 20.4 %fusion.48 = bf16[1,640,3456]{2,1,0:T(8,128)(2,1)} fusion(bf16[2048,3456]{1,0:T(8,128)(2,1)} %convolution_convert_fusion, f32[2048,3456]{1,0:T(8,128)} %fusion.71, bf16[1,2048,640]{1,2,0:T(8,128)(2,1)S(1)} %copy-done.2, f32[2048]{0:T(1024)S(1)} %copy-done.10), kind=kOutput, calls=%fused_computation.82 | convolution fusion | flops 9108307968 | bytes 49520640 | tf_op jit(solution)/shard_map/transpose(jvp())/dot_general | solution.py:22
  305.2 28.0 %fusion.43 = bf16[1,640,3456]{2,1,0:T(8,128)(2,1)} fusion(f32[2048,3456]{1,0:T(8,128)} %fusion.71, f32[2048,3456]{1,0:T(8,128)} %get-tuple-element.25, bf16[2048,3456]{1,0:T(8,128)(2,1)} %convolution_convert_fusion, bf16[1,2048,640]{1,2,0:T(8,128)(2,1)S(1)} %copy-done.2, f32[2048]{0:T(1024)S(1)} %copy-done.10), kind=kOutput, calls=%fused_computation.79 | convolution fusion | flops 9143697408 | bytes 77832192 | tf_op jit(solution)/shard_map/transpose(jvp())/dot_general | solution.py:21
  333.2 0.1 all-reduce.3.cloned.1.call-update
  333.2 269.2 %all-reduce.3.cloned.1.call-done = (bf16[1,640,3456]{2,1,0:T(8,128)(2,1)}, bf16[1,640,3456]{2,1,0:T(8,128)(2,1)}, bf16[1,640,3456]{2,1,0:T(8,128)(2,1)}, bf16[1,...) async-done(((bf16[1,640,3456]{2,1,0:T(8,128)(2,1)}, bf16[1,640,3456]{2,1,0:T(8,128)(2,1)}, bf16[1,640,3456]{2,1,0:T(8,128)(2,1)}, ...) | async-done | bytes 26542096 | tf_op jit(solution)/shard_map/psum | solution.py:50
  602.5 8.9 %fusion.24 = f32[]{:T(128)} fusion(bf16[1,3456,640]{2,1,0:T(8,128)(2,1)} %get-tuple-element.13, bf16[1,3456,640]{2,1,0:T(8,128)(2,1)} %get-tuple-element.14), kind=kLoop, calls=%fused_computation.48 | loop fusion | flops 17694720 | bytes 8847364 | tf_op jit(solution)/shard_map/reduce_sum | solution.py:52
  611.4 8.8 %fusion.23 = f32[]{:T(128)} fusion(bf16[1,640,3456]{2,1,0:T(8,128)(2,1)} %get-tuple-element.11, bf16[1,640,3456]{2,1,0:T(8,128)(2,1)} %get-tuple-element.12), kind=kLoop, calls=%fused_computation.47 | loop fusion | flops 17694720 | bytes 8847364 | tf_op jit(solution)/shard_map/reduce_sum | solution.py:52
  620.2 0.0 slice-done.4
  620.2 0.0 slice-start.2
  620.2 5.1 fusion.22
  627.3 0.0 slice-start.3
  627.3 34.1 %fusion.30 = (bf16[2,3456,640]{2,1,0:T(8,128)(2,1)}, f32[2,3456,640]{2,1,0:T(8,128)}, f32[2,3456,640]{2,1,0:T(8,128)}) fusion(bf16[2,3456,640]{2,1,0:T(8,128)(2,1)} %param.15, f32[]{:T(128)S(6)} %min_shard_map.3, bf16[1,3456,640]{2,1,0:T(8,128)(2,1)} %get-tuple-element.13, bf16[1,3456,640]{2,1,0:T(8,128)(2,1)} %get-tuple-element.14, ...), kind=kLoop, calls=%fused_computation.54 | loop fusion | flops 88473600 | bytes 97320960 | tf_op jit(solution)/shard_map/convert_element_type | solution.py:30
  661.5 0.0 slice-done.3
  661.5 59.2 %fusion.21 = (bf16[2,640,3456]{2,1,0:T(8,128)(2,1)}, f32[2,640,3456]{2,1,0:T(8,128)}, f32[2,640,3456]{2,1,0:T(8,128)}, bf16[2,640,3456]{2,1,0:T(8,128)(2,1)}, f3...) fusion(bf16[2,640,3456]{2,1,0:T(8,128)(2,1)} %param.13, f32[]{:T(128)S(6)} %min_shard_map.3, ...), kind=kLoop, calls=%fused_computation.45 | loop fusion | flops 176947200 | bytes 194641920 | tf_op jit(solution)/shard_map/convert_element_type | solution.py:30
  (26 shorter events, 0.1 us)
Async XLA Ops:
  7.2 595.3 %all-reduce.3.cloned.1.call-start = ((), (), s32[]{:S(2)}) async-start(), calls=%async_computation | async-start | bytes 53084160 | tf_op jit(solution)/shard_map/psum | solution.py:50
  10.3 70.5 %copy-start.1 = (bf16[1,2048,640]{1,2,0:T(8,128)(2,1)}, bf16[1,2048,640]{1,2,0:T(8,128)(2,1)S(1)}, u32[]{:S(2)}) copy-start(bf16[1,2048,640]{1,2,0:T(8,128)(2,1)S(1)} %copy.20) | copy-start | bytes 7864324
  10.8 39.8 %copy-start.9 = (f32[2048]{0:T(1024)}, f32[2048]{0:T(1024)S(1)}, u32[]{:S(2)}) copy-start(f32[2048]{0:T(1024)S(1)} %add_rsqrt_fusion) | copy-start | bytes 24580
  15.6 17.4 %copy-start.6 = (bf16[1,2048,640]{2,1,0:T(8,128)(2,1)S(1)}, bf16[1,2048,640]{2,1,0:T(8,128)(2,1)}, u32[]{:S(2)}) copy-start(bf16[1,2048,640]{2,1,0:T(8,128)(2,1)} %param.11) | copy-start | bytes 7864324
  95.4 0.6 copy-start.7
  95.4 1.5 copy-start.3
  172.7 25.0 %copy-start.4 = (bf16[2048,640]{0,1:T(8,128)(2,1)S(1)}, bf16[2048,640]{0,1:T(8,128)(2,1)}, u32[]{:S(2)}) copy-start(bf16[2048,640]{0,1:T(8,128)(2,1)} %copy-done.3) | copy-start | bytes 7864324
  197.7 15.0 %copy-start.8 = (f32[2048]{0:T(1024)S(1)}, f32[2048]{0:T(1024)}, u32[]{:S(2)}) copy-start(f32[2048]{0:T(1024)} %copy-done.7) | copy-start | bytes 24580
  197.7 15.0 %copy-start = (bf16[1,2048,640]{1,2,0:T(8,128)(2,1)S(1)}, bf16[1,2048,640]{1,2,0:T(8,128)(2,1)}, u32[]{:S(2)}) copy-start(bf16[1,2048,640]{1,2,0:T(8,128)(2,1)} %copy.21) | copy-start | bytes 7864324
  212.8 20.4 %slice-start.6 = ((s8[8847360]{0:T(1024)(128)(4,1)}), s8[4194304]{0:T(1024)(128)(4,1)S(1)}, s32[]{:S(2)}) async-start(s8[8847360]{0:T(1024)(128)(4,1)} %bitcast.86), calls=%async_computation.7 | async-start | bytes 8388608
  214.6 1.5 copy-start.5
  216.1 17.0 %slice-start.7 = ((s8[8847360]{0:T(1024)(128)(4,1)}), s8[4194304]{0:T(1024)(128)(4,1)S(1)}, s32[]{:S(2)}) async-start(s8[8847360]{0:T(1024)(128)(4,1)} %bitcast.86), calls=%async_computation.8 | async-start | bytes 8388608
  216.1 17.0 %slice-start.8 = ((s8[8847360]{0:T(1024)(128)(4,1)}), s8[458752]{0:T(1024)(128)(4,1)S(1)}, s32[]{:S(2)}) async-start(s8[8847360]{0:T(1024)(128)(4,1)} %bitcast.86), calls=%async_computation.9 | async-start | bytes 917504
  270.4 14.4 %copy-start.2 = (bf16[1,2048,640]{1,2,0:T(8,128)(2,1)S(1)}, bf16[1,2048,640]{1,2,0:T(8,128)(2,1)}, u32[]{:S(2)}) copy-start(bf16[1,2048,640]{1,2,0:T(8,128)(2,1)} %copy-done.1) | copy-start | bytes 7864324
  270.4 14.4 %copy-start.10 = (f32[2048]{0:T(1024)S(1)}, f32[2048]{0:T(1024)}, u32[]{:S(2)}) copy-start(f32[2048]{0:T(1024)} %copy-done.9) | copy-start | bytes 24580
  602.5 17.7 %slice-start = ((s8[4423680]{0:T(1024)(128)(4,1)}), s8[4194304]{0:T(1024)(128)(4,1)S(1)}, s32[]{:S(2)}) async-start(s8[4423680]{0:T(1024)(128)(4,1)} %bitcast.80), calls=%async_computation.1 | async-start | bytes 8388608
  602.5 17.7 %slice-start.4 = ((s8[4423680]{0:T(1024)(128)(4,1)}), s8[4194304]{0:T(1024)(128)(4,1)S(1)}, s32[]{:S(2)}) async-start(s8[4423680]{0:T(1024)(128)(4,1)} %bitcast.84), calls=%async_computation.5 | async-start | bytes 8388608
  611.4 8.8 %slice-start.1 = ((s8[4423680]{0:T(1024)(128)(4,1)}), s8[229376]{0:T(1024)(128)(4,1)S(1)}, s32[]{:S(2)}) async-start(s8[4423680]{0:T(1024)(128)(4,1)} %bitcast.80), calls=%async_computation.2 | async-start | bytes 458752
  611.4 8.8 %slice-start.5 = ((s8[4423680]{0:T(1024)(128)(4,1)}), s8[229376]{0:T(1024)(128)(4,1)S(1)}, s32[]{:S(2)}) async-start(s8[4423680]{0:T(1024)(128)(4,1)} %bitcast.84), calls=%async_computation.6 | async-start | bytes 458752
  620.2 41.3 %slice-start.2 = ((s8[4423680]{0:T(1024)(128)(4,1)}), s8[229376]{0:T(1024)(128)(4,1)S(1)}, s32[]{:S(2)}) async-start(s8[4423680]{0:T(1024)(128)(4,1)} %bitcast.82), calls=%async_computation.3 | async-start | bytes 458752
  627.3 34.1 %slice-start.3 = ((s8[4423680]{0:T(1024)(128)(4,1)}), s8[4194304]{0:T(1024)(128)(4,1)S(1)}, s32[]{:S(2)}) async-start(s8[4423680]{0:T(1024)(128)(4,1)} %bitcast.82), calls=%async_computation.4 | async-start | bytes 8388608
Sparse Core Ops, SparseCore 0:
  333.3 269.0 all-reduce.2
where the time goes:
time: 737 us; the launch traced here: 728 us
  matrix products  313 us (42%)
  waiting for transfers between devices  269 us (36%)
  other arithmetic  119 us (16%)
  between operations  16.7 us (2%)
  local copies, waits for them, and re-layouts  10.7 us (1%)
    psum x1, waiting for transfers between devices, step(): summed[number] = [lax.psum(by_w[name], 'dp') for name in NAMES]  269 us
    dot_general x5, matrix products, layer(): gate = jnp.dot(a, w['w_gate'], preferred_element_type=jnp.float32)  114 us
    dot_general x5, matrix products, layer(): up = jnp.dot(a, w['w_up'], preferred_element_type=jnp.float32)  108 us
    convert_element_type x2, other arithmetic, adamw(): return ((w - 0.02 * step).astype(jnp.bfloat16), m, v)  93.4 us
    dot_general x5, matrix products, matmul(): jnp.dot(a, w, preferred_element_type=jnp.float32).astype(jnp.bfloat16)  90.8 us
    reduce_sum x3, other arithmetic, step(): jnp.sum(g * g)  22.8 us
  transfers between devices with their start and end apart: 1, of which 1 were waited for; matrix products, arithmetic and copies ran while one was open for 0% of the time, Pallas kernels for 0%

commit v1 on v0

v1 whole, which is shorter than its diff:
```python
import functools
import jax
import jax.numpy as jnp
from jax import lax
from jax.experimental import pallas as pl
from jax.experimental.pallas import tpu as pltpu

F32, BF16 = jnp.float32, jnp.bfloat16
TILE = 512
CHUNK = 256


def nn(a, b):
    return jnp.dot(a, b, preferred_element_type=F32)


def nt(a, b):
    return lax.dot_general(a, b, (((1,), (1,)), ((), ())), preferred_element_type=F32)


def scale_of(wide):
    return lax.rsqrt(jnp.mean(wide * wide, -1, keepdims=True) + 1e-6)


def sigmoid(x):
    return 0.5 * jnp.tanh(0.5 * x) + 0.5


def rows_of(c):
    return pl.ds(pl.multiple_of(c * CHUNK, CHUNK), CHUNK)


def hold(ref, kept, axis, left):
    kept[...] = ref[0]
    if left < TILE:
        @pl.when(pl.program_id(0) == pl.num_programs(0) - 1)
        def _():
            if axis == 1:
                kept[:, left:] = jnp.zeros((kept.shape[0], TILE - left), kept.dtype)
            else:
                kept[left:, :] = jnp.zeros((TILE - left, kept.shape[1]), kept.dtype)


def forward_kernel(chunks, left, x_ref, wg_ref, wu_ref, wd_ref, h_ref, gate_ref, up_ref, a, acc, wg, wu, wd):
    j = pl.program_id(0)

    @pl.when(j == 0)
    def _():
        def norm(c, _):
            wide = x_ref[rows_of(c), :].astype(F32)
            a[rows_of(c), :] = (wide * scale_of(wide)).astype(BF16)
            acc[rows_of(c), :] = jnp.zeros((CHUNK, acc.shape[1]), F32)
            return _
        lax.fori_loop(0, chunks, norm, 0)

    hold(wg_ref, wg, 1, left)
    hold(wu_ref, wu, 1, left)
    hold(wd_ref, wd, 0, left)

    def body(c, _):
        r = rows_of(c)
        gate = nn(a[r, :], wg[...])
        up = nn(a[r, :], wu[...])
        gate_ref[r, :] = gate
        up_ref[r, :] = up
        act = (gate * sigmoid(gate) * up).astype(BF16)
        acc[r, :] += nn(act, wd[...])
        return _
    lax.fori_loop(0, chunks, body, 0)

    @pl.when(j == pl.num_programs(0) - 1)
    def _():
        def out(c, _):
            r = rows_of(c)
            h_ref[r, :] = (x_ref[r, :].astype(F32) + acc[r, :].astype(BF16).astype(F32)).astype(BF16)
            return _
        lax.fori_loop(0, chunks, out, 0)


def backward_kernel(chunks, left, last_layer, *refs):
    if last_layer:
        h_ref, dy_ref, wg_ref, wu_ref, wd_ref, g_ref, dh_ref, a, at, dyt, act, dgate, dup, acc, wg, wu, wd = refs
    else:
        h_ref, dy_ref, gate_ref, up_ref, wd_ref, g_ref, at, dyt, act, dgate, dup, wd = refs
    j = pl.program_id(0)

    @pl.when(j == 0)
    def _():
        def norm(c, _):
            r = rows_of(c)
            wide = h_ref[r, :].astype(F32)
            normed = (wide * scale_of(wide)).astype(BF16)
            at[:, r] = normed.T
            dyt[:, r] = dy_ref[r, :].T
            if last_layer:
                a[r, :] = normed
                acc[r, :] = jnp.zeros((CHUNK, acc.shape[1]), F32)
            return _
        lax.fori_loop(0, chunks, norm, 0)

    if last_layer:
        hold(wg_ref, wg, 1, left)
        hold(wu_ref, wu, 1, left)
    hold(wd_ref, wd, 0, left)

    def body(c, _):
        r = rows_of(c)
        if last_layer:
            gate = nn(a[r, :], wg[...])
            up = nn(a[r, :], wu[...])
        else:
            gate = gate_ref[r, :]
            up = up_ref[r, :]
        d = nt(dy_ref[r, :], wd[...]).astype(BF16).astype(F32)
        s = sigmoid(gate)
        silu = gate * s
        act[r, :] = (silu * up).astype(BF16)
        d_up = (d * silu).astype(BF16)
        d_gate = (d * up * (s + silu * (1.0 - s))).astype(BF16)
        dup[r, :] = d_up
        dgate[r, :] = d_gate
        if last_layer:
            acc[r, :] += nt(d_gate, wg[...]) + nt(d_up, wu[...])
        return _
    lax.fori_loop(0, chunks, body, 0)

    g_ref[:, 0:TILE] = nn(at[...], dgate[...]).astype(BF16)
    g_ref[:, TILE : 2 * TILE] = nn(at[...], dup[...]).astype(BF16)
    g_ref[:, 2 * TILE : 3 * TILE] = nn(dyt[...], act[...]).astype(BF16)

    if last_layer:
        @pl.when(j == pl.num_programs(0) - 1)
        def _():
            def out(c, _):
                r = rows_of(c)
                wide = h_ref[r, :].astype(F32)
                scale = scale_of(wide)
                da = acc[r, :].astype(BF16).astype(F32)
                dot = jnp.mean(da * wide, -1, keepdims=True)
                by = scale * da - wide * (scale * scale * scale * dot)
                dh_ref[r, :] = (dy_ref[r, :].astype(F32) + by.astype(BF16).astype(F32)).astype(BF16)
                return _
            lax.fori_loop(0, chunks, out, 0)


def whole(shape):
    return pl.BlockSpec(shape, lambda j: (0,) * len(shape))


def params():
    return pltpu.CompilerParams(dimension_semantics=("arbitrary",), vmem_limit_bytes=62 * 1024 * 1024)


def forward(x, w, layer):
    tokens, d = x.shape
    ff = w[0].shape[2]
    tiles = pl.cdiv(ff, TILE)
    col = pl.BlockSpec((1, d, TILE), lambda j: (layer, 0, j))
    row = pl.BlockSpec((1, TILE, d), lambda j: (layer, j, 0))
    saved = pl.BlockSpec((tokens, TILE), lambda j: (0, j))
    return pl.pallas_call(
        functools.partial(forward_kernel, tokens // CHUNK, ff - (tiles - 1) * TILE),
        grid=(tiles,),
        in_specs=[whole((tokens, d)), col, col, row],
        out_specs=[whole((tokens, d)), saved, saved],
        out_shape=[jax.ShapeDtypeStruct((tokens, d), BF16)] + [jax.ShapeDtypeStruct((tokens, tiles * TILE), F32)] * 2,
        scratch_shapes=[pltpu.VMEM((tokens, d), BF16), pltpu.VMEM((tokens, d), F32), pltpu.VMEM((d, TILE), BF16), pltpu.VMEM((d, TILE), BF16), pltpu.VMEM((TILE, d), BF16)],
        compiler_params=params(),
        cost_estimate=pl.CostEstimate(flops=6 * tokens * d * ff, bytes_accessed=8 * tokens * ff, transcendentals=tokens * ff),
        name="forward",
    )(x, *w)


def backward_last(h, dy, w, layer):
    tokens, d = h.shape
    ff = w[0].shape[2]
    tiles = pl.cdiv(ff, TILE)
    col = pl.BlockSpec((1, d, TILE), lambda j: (layer, 0, j))
    row = pl.BlockSpec((1, TILE, d), lambda j: (layer, j, 0))
    return pl.pallas_call(
        functools.partial(backward_kernel, tokens // CHUNK, ff - (tiles - 1) * TILE, True),
        grid=(tiles,),
        in_specs=[whole((tokens, d)), whole((tokens, d)), col, col, row],
        out_specs=[pl.BlockSpec((d, 3 * TILE), lambda j: (0, j)), whole((tokens, d))],
        out_shape=[jax.ShapeDtypeStruct((d, 3 * TILE * tiles), BF16), jax.ShapeDtypeStruct((tokens, d), BF16)],
        scratch_shapes=[pltpu.VMEM((tokens, d), BF16)] + [pltpu.VMEM((d, tokens), BF16)] * 2 + [pltpu.VMEM((tokens, TILE), BF16)] * 3
        + [pltpu.VMEM((tokens, d), F32), pltpu.VMEM((d, TILE), BF16), pltpu.VMEM((d, TILE), BF16), pltpu.VMEM((TILE, d), BF16)],
        compiler_params=params(),
        cost_estimate=pl.CostEstimate(flops=16 * tokens * d * ff, bytes_accessed=12 * d * ff, transcendentals=tokens * ff),
        name="backward_last",
    )(h, dy, *w)


def backward_first(h, dy, gate, up, wd, layer):
    tokens, d = h.shape
    ff = wd.shape[1]
    tiles = pl.cdiv(ff, TILE)
    row = pl.BlockSpec((1, TILE, d), lambda j: (layer, j, 0))
    saved = pl.BlockSpec((tokens, TILE), lambda j: (0, j))
    return pl.pallas_call(
        functools.partial(backward_kernel, tokens // CHUNK, ff - (tiles - 1) * TILE, False),
        grid=(tiles,),
        in_specs=[whole((tokens, d)), whole((tokens, d)), saved, saved, row],
        out_specs=pl.BlockSpec((d, 3 * TILE), lambda j: (0, j)),
        out_shape=jax.ShapeDtypeStruct((d, 3 * TILE * tiles), BF16),
        scratch_shapes=[pltpu.VMEM((d, tokens), BF16)] * 2 + [pltpu.VMEM((tokens, TILE), BF16)] * 3 + [pltpu.VMEM((TILE, d), BF16)],
        compiler_params=params(),
        cost_estimate=pl.CostEstimate(flops=8 * tokens * d * ff, bytes_accessed=8 * tokens * ff, transcendentals=tokens * ff),
        name="backward_first",
    )(h, dy, gate, up, wd)


def adamw_kernel(fresh, factor_ref, g_ref, *refs):
    w_refs, m_refs, v_refs = refs[0:3], refs[3:6], refs[6:9]
    outs = refs[9:] if fresh else refs[18:]
    factor = factor_ref[0, 0]
    for i in range(3):
        g = g_ref[:, i * TILE : (i + 1) * TILE].astype(F32) * factor
        if i == 2:
            g = g.T
        m = 0.9 * m_refs[i][0] + 0.1 * g
        v = 0.95 * v_refs[i][0] + 0.05 * g * g
        w = w_refs[i][0].astype(F32)
        outs[i][0] = (w - 0.02 * (m * lax.rsqrt(v + 1e-8) + 0.1 * w)).astype(BF16)
        outs[3 + i][0] = m
        outs[6 + i][0] = v


def adamw(factor, g, w, m, v, layer, so_far=None):
    layers, d, ff = w[0].shape
    tiles = pl.cdiv(ff, TILE)
    col = pl.BlockSpec((1, d, TILE), lambda j: (layer, 0, j))
    row = pl.BlockSpec((1, TILE, d), lambda j: (layer, j, 0))
    nine = [col, col, row] * 3
    arrays = [*w, *m, *v]
    held = [] if so_far is None else list(so_far)
    return pl.pallas_call(
        functools.partial(adamw_kernel, so_far is None),
        grid=(tiles,),
        in_specs=[pl.BlockSpec(memory_space=pltpu.SMEM), pl.BlockSpec((d, 3 * TILE), lambda j: (0, j))] + nine + [pl.BlockSpec(memory_space=pl.ANY)] * len(held),
        out_specs=nine,
        out_shape=[jax.ShapeDtypeStruct(a.shape, a.dtype) for a in arrays],
        input_output_aliases={11 + i: i for i in range(len(held))},
        compiler_params=params(),
        cost_estimate=pl.CostEstimate(flops=60 * d * ff, bytes_accessed=66 * d * ff, transcendentals=3 * d * ff),
        name="adamw",
    )(factor, g, *arrays, *held)


def solution(mesh):
    from jax.sharding import PartitionSpec as P

    def step(x, dy, *arrays):
        w, m, v = (arrays[i : i + 3] for i in (0, 3, 6))
        x, dy = x[0], dy[0]
        h, gate, up = forward(x, w, 0)
        g1, dh = backward_last(h, dy, w, 1)
        s1 = lax.psum_scatter(g1, "dp", scatter_dimension=0, tiled=True)
        g0 = backward_first(x, dh, gate, up, w[2], 0)
        s0 = lax.psum_scatter(g0, "dp", scatter_dimension=0, tiled=True)
        squares = sum(jnp.sum(s.astype(F32) ** 2) for s in (s1, s0))
        squares = lax.psum(squares, "dp")
        count = sum(a.size for a in w)
        factor = jnp.minimum(1.0, 0.5 * lax.rsqrt(squares / count + 1e-30)).reshape(1, 1)
        t1 = lax.all_gather(s1, "dp", axis=0, tiled=True)
        t0 = lax.all_gather(s0, "dp", axis=0, tiled=True)
        new = adamw(factor, t1, w, m, v, 1)
        return tuple(adamw(factor, t0, w, m, v, 0, new))

    return jax.shard_map(
        step,
        mesh=mesh,
        in_specs=(P(("rep", "dp"), None, None),) * 2 + (P(None, None, None),) * 9,
        out_specs=(P("rep", None, None),) * 9,
        check_vma=False,
    )
```

time: 737 us -> 539 us (0.73); the launches traced: 728 us -> 539 us
  Pallas kernels: 0 us -> 356 us
  matrix products: 313 us -> 0 us
  waiting for transfers between devices: 269 us -> 146 us
  other arithmetic: 119 us -> 5.9 us
  blocking collectives: 0 us -> 14.3 us
  local copies, waits for them, and re-layouts: 10.7 us -> 0 us
    pallas_call x0 -> x5, Pallas kernels: none -> 356 us  [the longest x1 116 us: backward_last(): pl.pallas_call(functools.partial(backward_kernel, tokens // CHUNK, ff - (...]
    dot_general x15 -> x0, matrix products: 313 us -> none  [the longest x5 114 us: layer(): gate = jnp.dot(a, w['w_gate'], preferred_element_type=jnp.float32)]
    psum x1 -> x0, waiting for transfers between devices: 269 us -> none  [step(): summed[number] = [lax.psum(by_w[name], 'dp') for name in NAMES]]
    convert_element_type x2 -> x0, other arithmetic: 93.4 us -> none  [adamw(): return ((w - 0.02 * step).astype(jnp.bfloat16), m, v)]
    reduce_scatter x0 -> x2, waiting for transfers between devices: none -> 83.7 us  [the longest x1 76.4 us: step(): s0 = lax.psum_scatter(g0, 'dp', scatter_dimension=0, tiled=True)]
    all_gather x0 -> x2, waiting for transfers between devices: none -> 62.5 us  [the longest x1 48.4 us: step(): t1 = lax.all_gather(s1, 'dp', axis=0, tiled=True)]
    reduce_sum x4 -> x2, other arithmetic: 23.4 us -> 5.9 us  [step(): squares = sum((jnp.sum(s.astype(F32) ** 2) for s in (s1, s0)))]
    psum x0 -> x1, blocking collectives: none -> 14.3 us  [step(): squares = lax.psum(squares, 'dp')]
  transfers between devices with their start and end apart: 1 -> 4, of which waited for: 1 -> 4; matrix products, arithmetic and copies ran while one was open for 0% -> 1% of each run, Pallas kernels for 0% -> 23%
where the time goes in v1:
time: 539 us
  Pallas kernels  356 us (66%)
  waiting for transfers between devices  146 us (27%)
  between operations  15.8 us (3%)
  blocking collectives  14.3 us (3%)
  other arithmetic  5.9 us (1%)
    pallas_call x1, Pallas kernels, backward_last(): pl.pallas_call(functools.partial(backward_kernel, tokens // CHUNK, ff - (...  116 us
    pallas_call x2, Pallas kernels, adamw(): pl.pallas_call(functools.partial(adamw_kernel, so_far is None), grid=(til...  112 us
    reduce_scatter x1, waiting for transfers between devices, step(): s0 = lax.psum_scatter(g0, 'dp', scatter_dimension=0, tiled=True)  76.4 us
    pallas_call x1, Pallas kernels, backward_first(): pl.pallas_call(functools.partial(backward_kernel, tokens // CHUNK, ff - (...  69.1 us
    pallas_call x1, Pallas kernels, forward(): pl.pallas_call(functools.partial(forward_kernel, tokens // CHUNK, ff - (t...  59.1 us
    all_gather x1, waiting for transfers between devices, step(): t1 = lax.all_gather(s1, 'dp', axis=0, tiled=True)  48.4 us
    psum x1, blocking collectives, step(): squares = lax.psum(squares, 'dp')  14.3 us
    all_gather x1, waiting for transfers between devices, step(): t0 = lax.all_gather(s0, 'dp', axis=0, tiled=True)  14.2 us
  transfers between devices with their start and end apart: 4, of which 4 were waited for; matrix products, arithmetic and copies ran while one was open for 1% of the time, Pallas kernels for 23%

profile of v1, /device:TPU:113, one launch (start us, length us, event | category | flops | bytes accessed | tf_op | source)
XLA Modules:
  0.0 538.5 jit_solution(10897267552824192560)
XLA Ops:
  7.2 0.1 reduce-scatter.3.cloned.1.call-start
  7.3 59.1 %forward.1 = (bf16[2048,640]{1,0:T(8,128)(2,1)}, f32[2048,3584]{1,0:T(8,128)}, f32[2048,3584]{1,0:T(8,128)}) custom-call(bf16[2048,640]{1,0:T(8,128)(2,1)} %bitcast.4, bf16[2,640,3456]{2,1,0:T(8,128)(2,1)} %refs_0_.3, bf16[2,640,3456]{2,1,0:T(8,128)(2,1)} %refs_1_.3, bf16[2,3456,640]{2,1,0:T(8,128)(2,1)} %refs_2_.5), custom_call_target="tpu_custom_call" | custom-call | flops 27179089920 | bytes 56623104 | tf_op jit(solution)/shard_map/forward/pallas_call | solution.py:161
  66.3 115.9 %backward_last.1 = (bf16[640,10752]{1,0:T(8,128)(2,1)}, bf16[2048,640]{1,0:T(8,128)(2,1)}) custom-call(bf16[2048,640]{1,0:T(8,128)(2,1)} %get-tuple-element.23.refs_0_, bf16[2048,640]{1,0:T(8,128)(2,1)} %bitcast.3, bf16[2,640,3456]{2,1,0:T(8,128)(2,1)} %refs_0_.3, bf16[2,640,3456]{2,1,0:T(8,128)(2,1)} %refs_1_.3, bf16[2,3456,640]{2,1,0:T(8,128)(2,1)} %refs_2_.5), custom_call_target="tpu_custom_call" | custom-call | flops 72477573120 | bytes 26542080 | tf_op jit(solution)/shard_map/backward_last/pallas_call | solution.py:180
  182.2 0.1 reduce-scatter.3.cloned.1.call-update
  182.3 0.1 reduce-scatter.5.cloned.1.call-start
  182.4 69.1 %backward_first.1 = bf16[640,10752]{1,0:T(8,128)(2,1)} custom-call(bf16[2048,640]{1,0:T(8,128)(2,1)} %bitcast.5, bf16[2048,640]{1,0:T(8,128)(2,1)} %get-tuple-element.25.refs_1_, f32[2048,3584]{1,0:T(8,128)} %get-tuple-element.26.refs_2_, f32[2048,3584]{1,0:T(8,128)} %get-tuple-element.27.refs_3_, bf16[2,3456,640]{2,1,0:T(8,128)(2,1)} %refs_2_.5), custom_call_target="tpu_custom_call" | custom-call | flops 36238786560 | bytes 56623104 | tf_op jit(solution)/shard_map/backward_first/pallas_call | solution.py:200
  251.5 0.1 reduce-scatter.5.cloned.1.call-update
  251.6 0.1 all-gather.5.cloned.1.call-start
  251.6 7.3 %reduce-scatter.3.cloned.1.call-done = bf16[80,10752]{1,0:T(8,128)(2,1)} async-done(((bf16[640,10752]{1,0:T(8,128)(2,1)}), bf16[80,10752]{1,0:T(8,128)(2,1)}) %reduce-scatter.3.cloned.1.call-update) | async-done | bytes 1720336 | tf_op jit(solution)/shard_map/reduce_scatter | solution.py:258
  258.9 0.1 all-gather.5.cloned.1.call-update
  259.0 0.1 all-gather.3.cloned.1.call-start
  259.0 76.4 %reduce-scatter.5.cloned.1.call-done = bf16[80,10752]{1,0:T(8,128)(2,1)} async-done(((bf16[640,10752]{1,0:T(8,128)(2,1)}), bf16[80,10752]{1,0:T(8,128)(2,1)}) %reduce-scatter.5.cloned.1.call-update) | async-done | bytes 1720336 | tf_op jit(solution)/shard_map/reduce_scatter | solution.py:260
  335.4 0.1 all-gather.3.cloned.1.call-update
  335.5 2.9 multiply_reduce_fusion.1
  338.5 2.9 multiply_reduce_fusion
  342.7 14.3 %psum.7 = f32[]{:T(128)} all-reduce(f32[]{:T(128)S(6)} %add.12), channel_id=1, replica_groups=mesh['rep'=2,'dp'=8] {'dp'}, use_global_device_ids=true, to_apply=%region_4.0 | all-reduce | flops 1 | bytes 8 | tf_op jit(solution)/shard_map/psum | solution.py:262
  357.7 48.4 %all-gather.5.cloned.1.call-done.g_ref = bf16[640,10752]{1,0:T(8,128)(2,1)} async-done(((bf16[80,10752]{1,0:T(8,128)(2,1)}), bf16[640,10752]{1,0:T(8,128)(2,1)}) %all-gather.5.cloned.1.call-update) | async-done | bytes 13762576 | tf_op jit(solution)/shard_map/all_gather | solution.py:265
  406.0 55.9 %adamw.2 = (bf16[2,640,3456]{2,1,0:T(8,128)(2,1)}, bf16[2,640,3456]{2,1,0:T(8,128)(2,1)}, bf16[2,3456,640]{2,1,0:T(8,128)(2,1)}, f32[2,640,3456]{2,1,0:T(8,128)}...) custom-call(f32[1,1]{1,0:T(1,128)} %bitcast.2.factor_ref, ...), custom_call_target="tpu_custom_call" | custom-call | flops 132710400 | bytes 145981440 | tf_op jit(solution)/shard_map/adamw/pallas_call | solution.py:237
  461.9 14.2 %all-gather.3.cloned.1.call-done.g_ref = bf16[640,10752]{1,0:T(8,128)(2,1)} async-done(((bf16[80,10752]{1,0:T(8,128)(2,1)}), bf16[640,10752]{1,0:T(8,128)(2,1)}) %all-gather.3.cloned.1.call-update) | async-done | bytes 13762576 | tf_op jit(solution)/shard_map/all_gather | solution.py:266
  476.1 55.8 %adamw.3 = (bf16[2,640,3456]{2,1,0:T(8,128)(2,1)}, bf16[2,640,3456]{2,1,0:T(8,128)(2,1)}, bf16[2,3456,640]{2,1,0:T(8,128)(2,1)}, f32[2,640,3456]{2,1,0:T(8,128)}...) custom-call(f32[1,1]{1,0:T(1,128)} %bitcast.2.factor_ref, ...), custom_call_target="tpu_custom_call", output_to_operand_aliasing={{0}: (11, {}), {1}: (12, {}), {2}: (13, {}), {3}: (14, {}),... | custom-call | flops 132710400 | bytes 145981440 | tf_op jit(solution)/shard_map/adamw/pallas_call | solution.py:237
Async XLA Ops:
  7.2 251.7 %reduce-scatter.3.cloned.1.call-start = ((), (), s32[]{:S(2)}) async-start(), calls=%async_computation.2 | async-start | bytes 15482880 | tf_op jit(solution)/shard_map/reduce_scatter | solution.py:258
  182.3 153.1 %reduce-scatter.5.cloned.1.call-start = ((), (), s32[]{:S(2)}) async-start(), calls=%async_computation.3 | async-start | bytes 15482880 | tf_op jit(solution)/shard_map/reduce_scatter | solution.py:260
  251.6 154.5 %all-gather.5.cloned.1.call-start = ((), (), s32[]{:S(2)}) async-start(), calls=%async_computation.5 | async-start | bytes 15482880 | tf_op jit(solution)/shard_map/all_gather | solution.py:265
  259.0 217.1 %all-gather.3.cloned.1.call-start = ((), (), s32[]{:S(2)}) async-start(), calls=%async_computation.4 | async-start | bytes 15482880 | tf_op jit(solution)/shard_map/all_gather | solution.py:266
Sparse Core Ops, SparseCore 0:
  182.4 76.4 reduce-scatter.2
  261.8 73.6 reduce-scatter.4
  337.0 68.9 all-gather.4
  407.5 68.5 all-gather.2

commit v2 on v1

v2 whole, which is shorter than its diff:
```python
import functools
import jax
import jax.numpy as jnp
from jax import lax
from jax.experimental import pallas as pl
from jax.experimental.pallas import tpu as pltpu
from jax.sharding import PartitionSpec as P

F32, BF16 = jnp.float32, jnp.bfloat16
TILE = 512
CHUNK = 1024
WIDE = 2048
SLOTS, HALF_SLOTS, RING_SLOTS = 4, 6, 3
MESH = pl.DeviceIdType.MESH


def nn(a, b):
    return jnp.dot(a, b, preferred_element_type=F32)


def nt(a, b):
    return lax.dot_general(a, b, (((1,), (1,)), ((), ())), preferred_element_type=F32)


def scale_of(wide):
    return lax.rsqrt(jnp.mean(wide * wide, -1, keepdims=True) + 1e-6)


def sigmoid(x):
    return 0.5 * jnp.tanh(0.5 * x) + 0.5


def rows_of(c):
    return pl.ds(pl.multiple_of(c * CHUNK, CHUNK), CHUNK)


def hold(ref, kept, axis, left, at_end):
    kept[...] = ref[0]
    if left < TILE:
        @pl.when(at_end)
        def _():
            if axis == 1:
                kept[:, left:] = jnp.zeros((kept.shape[0], TILE - left), kept.dtype)
            else:
                kept[left:, :] = jnp.zeros((TILE - left, kept.shape[1]), kept.dtype)


def forward_kernel(chunks, left, x_ref, wg_ref, wu_ref, wd_ref, h_ref, at_ref, gate_ref, up_ref, a, acc, wg, wu, wd):
    j = pl.program_id(0)

    @pl.when(j == 0)
    def _():
        def norm(c, _):
            wide = x_ref[rows_of(c), :].astype(F32)
            normed = (wide * scale_of(wide)).astype(BF16)
            a[rows_of(c), :] = normed
            at_ref[:, rows_of(c)] = normed.T
            acc[rows_of(c), :] = jnp.zeros((CHUNK, acc.shape[1]), F32)
            return _
        lax.fori_loop(0, chunks, norm, 0)

    hold(wg_ref, wg, 1, left, j == pl.num_programs(0) - 1)
    hold(wu_ref, wu, 1, left, j == pl.num_programs(0) - 1)
    hold(wd_ref, wd, 0, left, j == pl.num_programs(0) - 1)

    def body(c, _):
        r = rows_of(c)
        gate = nn(a[r, :], wg[...])
        up = nn(a[r, :], wu[...])
        gate_ref[r, :] = gate
        up_ref[r, :] = up
        act = (gate * sigmoid(gate) * up).astype(BF16)
        acc[r, :] += nn(act, wd[...])
        return _
    lax.fori_loop(0, chunks, body, 0)

    @pl.when(j == pl.num_programs(0) - 1)
    def _():
        def out(c, _):
            r = rows_of(c)
            h_ref[r, :] = (x_ref[r, :].astype(F32) + acc[r, :].astype(BF16).astype(F32)).astype(BF16)
            return _
        lax.fori_loop(0, chunks, out, 0)


def place():
    chips = lax.axis_size("dp") // 2
    me = lax.axis_index("dp")
    chip, core = me // 2, lax.rem(me, 2)
    right, left = lax.rem(chip + 1, chips), lax.rem(chip + chips - 1, chips)
    return chips, chip, core, right, left, lax.rem(chip + 2, chips)


def wide_sum(*terms):
    total = terms[0].astype(F32)
    for term in terms[1:]:
        total = total + term.astype(F32)
    return total


class Exchange:
    def __init__(self, tiles, gathered, all_ref, own_ref, g, half, near, far, own, squares, send, recv, local):
        self.tiles, self.gathered, self.all_ref, self.own_ref = tiles, gathered, all_ref, own_ref
        self.g, self.half, self.near, self.far, self.own, self.squares = g, half, near, far, own, squares
        self.send, self.recv, self.local = send, recv, local
        self.chips, self.chip, self.core, self.right, self.left, self.across = place()
        self.depth, self.width = own.shape[1], own.shape[2]
        self.mid = self.width // 2

    def copy(self, kind, t, src, dst, chip=None, core=None):
        to = (self.chip if chip is None else chip) * 2 + (self.core if core is None else core)
        return pltpu.make_async_remote_copy(
            src_ref=src, dst_ref=dst, send_sem=self.send.at[kind, t], recv_sem=self.recv.at[kind, t], device_id={"dp": to}, device_id_type=MESH
        )

    def rows(self, chip, core=None):
        core = self.core if core is None else core
        return pl.ds(pl.multiple_of((core * self.chips + chip) * self.depth, 16), self.depth)

    def within(self, chip):
        return pl.ds(pl.multiple_of(chip * self.depth, 16), self.depth)

    def swap(self, t):
        theirs = pl.ds(pl.multiple_of((1 - self.core) * self.chips * self.depth, 16), self.chips * self.depth)
        return self.copy(0, t, self.g.at[lax.rem(t, SLOTS), theirs, :], self.half.at[lax.rem(t, HALF_SLOTS)], core=1 - self.core)

    def first(self, t):
        slot, r = lax.rem(t, SLOTS), self.rows(self.across)
        return (
            self.copy(1, t, self.g.at[slot, r, pl.ds(0, self.mid)], self.near.at[0, lax.rem(t, RING_SLOTS)], chip=self.right),
            self.copy(2, t, self.g.at[slot, r, pl.ds(self.mid, self.mid)], self.near.at[1, lax.rem(t, RING_SLOTS)], chip=self.left),
        )

    def second(self, t):
        slot = lax.rem(t, SLOTS)
        return (
            self.copy(3, t, self.g.at[slot, self.rows(self.right), :], self.far.at[0, lax.rem(t, RING_SLOTS)], chip=self.right),
            self.copy(4, t, self.g.at[slot, self.rows(self.left), :], self.far.at[1, lax.rem(t, RING_SLOTS)], chip=self.left),
        )

    def cols(self, t, start=0, size=None):
        return pl.ds(pl.multiple_of(t * self.width + start, 128), self.width if size is None else size)

    def region(self, chip, t, start=0, size=None):
        return self.all_ref.at[self.rows(chip), self.cols(t, start, size)]

    def spread(self, t):
        there = self.region(self.chip, t)
        return (
            self.copy(5, t, self.own.at[t], there, chip=self.right),
            self.copy(6, t, self.own.at[t], there, chip=self.left),
            self.copy(7, t, self.own.at[t], there, core=1 - self.core),
        )

    def onward(self, t):
        one, two = self.region(self.left, t, 0, self.mid), self.region(self.right, t, self.mid, self.mid)
        return (self.copy(8, t, one, one, chip=self.right), self.copy(9, t, two, two, chip=self.left))

    def across_chip(self, t):
        one, two = self.region(self.left, t), self.region(self.right, t)
        return (self.copy(10, t, one, one, core=1 - self.core), self.copy(11, t, two, two, core=1 - self.core))

    def last(self, t):
        it = self.region(self.across, t)
        return self.copy(12, t, it, it, core=1 - self.core)

    def kept(self, t):
        return pltpu.make_async_copy(self.own.at[t], self.region(self.chip, t), self.local.at[t])

    def kept_alone(self, t):
        return pltpu.make_async_copy(self.own.at[t], self.own_ref.at[:, self.cols(t - self.gathered)], self.local.at[t])

    def stage(self, j, lag, what, start, stop):
        t = j - lag

        @pl.when((t >= start) & (t < stop))
        def _():
            what(t)

    def step(self, j):
        everyone, alone = (0, self.gathered), (self.gathered, self.tiles)
        self.stage(j, 0, lambda t: self.swap(t).start(), 0, self.tiles)
        self.stage(j, 6, self.finish, *everyone)
        self.stage(j, 5, self.forward_far, *everyone)
        self.stage(j, 4, self.forward_near, *everyone)
        self.stage(j, 4, lambda t: self.kept_alone(t).wait(), *alone)
        self.stage(j, 3, self.own_block, 0, self.tiles)
        self.stage(j, 2, self.neighbours, 0, self.tiles)
        self.stage(j, 1, self.far_block, 0, self.tiles)

    def far_block(self, t):
        self.swap(t).wait_recv()
        slot, r = lax.rem(t, SLOTS), self.rows(self.across)
        self.g[slot, r, :] = wide_sum(self.g[slot, r, :], self.half[lax.rem(t, HALF_SLOTS), self.within(self.across), :]).astype(BF16)
        for one in self.first(t):
            one.start()

    def neighbours(self, t):
        slot, mid = lax.rem(t, SLOTS), self.mid
        for one in self.first(t):
            one.wait_recv()
        for chip, side in ((self.right, 0), (self.left, 1)):
            r, h = self.rows(chip), self.within(chip)
            met, other = pl.ds(side * mid, mid), pl.ds((1 - side) * mid, mid)
            self.g[slot, r, met] = wide_sum(self.g[slot, r, met], self.half[lax.rem(t, HALF_SLOTS), h, met], self.near[side, lax.rem(t, RING_SLOTS)]).astype(BF16)
            self.g[slot, r, other] = wide_sum(self.g[slot, r, other], self.half[lax.rem(t, HALF_SLOTS), h, other]).astype(BF16)
        for one in self.second(t):
            one.start()

    def own_block(self, t):
        slot = lax.rem(t, SLOTS)
        for one in self.second(t):
            one.wait_recv()
        total = wide_sum(self.g[slot, self.rows(self.chip), :], self.half[lax.rem(t, HALF_SLOTS), self.within(self.chip), :], self.far[0, lax.rem(t, RING_SLOTS)], self.far[1, lax.rem(t, RING_SLOTS)]).astype(BF16)
        self.own[t] = total
        wide = total.astype(F32)
        self.squares[...] += jnp.sum((wide * wide).reshape(-1, 8, 128), axis=0)

        @pl.when(t < self.gathered)
        def _():
            self.kept(t).start()
            for one in self.spread(t):
                one.start()

        @pl.when(t >= self.gathered)
        def _():
            self.kept_alone(t).start()

        for one in (self.swap(t), *self.first(t), *self.second(t)):
            one.wait_send()

    def forward_near(self, t):
        right, left, _ = self.spread(t)
        right.wait_recv()
        left.wait_recv()
        for one in (*self.onward(t), *self.across_chip(t)):
            one.start()

    def forward_far(self, t):
        for one in self.onward(t):
            one.wait_recv()
        self.last(t).start()

    def finish(self, t):
        self.kept(t).wait()
        right, left, other = self.spread(t)
        other.wait_recv()
        for one in self.across_chip(t):
            one.wait_recv()
        self.last(t).wait_recv()
        for one in (right, left, other, *self.onward(t), *self.across_chip(t), self.last(t)):
            one.wait_send()


def greet(everyone):
    chips, chip, core, right, left, _ = place()
    barrier = pltpu.get_barrier_semaphore()
    if everyone:
        me = lax.axis_index("dp")
        others = [lax.rem(me + k, 2 * chips) for k in range(1, 2 * chips)]
    else:
        others = [right * 2 + core, left * 2 + core, chip * 2 + 1 - core]
    for other in others:
        pl.semaphore_signal(barrier, inc=1, device_id={"dp": other}, device_id_type=MESH)
    pl.semaphore_wait(barrier, len(others))


def tile_gradients(g, slot, at, dyt, dgate, dup, act):
    g[slot, :, 0:TILE] = nn(at[...], dgate[...]).astype(BF16)
    g[slot, :, TILE : 2 * TILE] = nn(at[...], dup[...]).astype(BF16)
    g[slot, :, 2 * TILE : 3 * TILE] = nn(dyt[...], act[...]).astype(BF16)


def activations(gate, up, d, act, dgate, dup, r):
    s = sigmoid(gate)
    silu = gate * s
    act[r, :] = (silu * up).astype(BF16)
    d_up = (d * silu).astype(BF16)
    d_gate = (d * up * (s + silu * (1.0 - s))).astype(BF16)
    dup[r, :] = d_up
    dgate[r, :] = d_gate
    return d_gate, d_up


def backward_kernel(tiles, left, count, h_ref, dy_ref, at_ref, gate_ref, up_ref, wg_ref, wu_ref, wd_ref, all_ref, own_ref, factor_ref,
                    a, at, dyt, act, dgate, dup, wide, wg, wu, wd, loaded, all_squares, sent, arrived, *comm):
    j = pl.program_id(0)
    d = h_ref.shape[1]
    tokens = h_ref.shape[0]
    exchange = Exchange(2 * tiles, tiles, all_ref, own_ref, *comm)
    at_end = (j == tiles - 1) | (j == 2 * tiles - 1)
    acc = wide.at[:, 0:d]

    def saved(i):
        cols = pl.ds(pl.multiple_of(i * TILE, 128), TILE)
        return (
            pltpu.make_async_copy(gate_ref.at[:, cols], wide.at[:, 0:TILE], loaded.at[0]),
            pltpu.make_async_copy(up_ref.at[:, cols], wide.at[:, TILE : 2 * TILE], loaded.at[1]),
        )

    @pl.when(j == 0)
    def _():
        greet(True)
        exchange.squares[...] = jnp.zeros_like(exchange.squares)

        def norm(c, _):
            r = rows_of(c)
            x = h_ref[r, :].astype(F32)
            normed = (x * scale_of(x)).astype(BF16)
            at[:, r] = normed.T
            dyt[:, r] = dy_ref[r, :].T
            a[r, :] = normed
            acc[r, :] = jnp.zeros((CHUNK, d), F32)
            return _
        lax.fori_loop(0, tokens // CHUNK, norm, 0)

    @pl.when(j < tiles)
    def _():
        hold(wg_ref, wg, 1, left, at_end)
        hold(wu_ref, wu, 1, left, at_end)
        hold(wd_ref, wd, 0, left, at_end)

        def body(c, _):
            r = rows_of(c)
            gate = nn(a[r, :], wg[...])
            up = nn(a[r, :], wu[...])
            d = nt(dy_ref[r, :], wd[...]).astype(BF16).astype(F32)
            d_gate, d_up = activations(gate, up, d, act, dgate, dup, r)
            acc[r, :] += nt(d_gate, wg[...]) + nt(d_up, wu[...])
            return _
        lax.fori_loop(0, tokens // CHUNK, body, 0)

    @pl.when(j == tiles)
    def _():
        normed = pltpu.make_async_copy(at_ref, at, loaded.at[2])
        normed.start()

        def out(c, _):
            r = rows_of(c)
            x = h_ref[r, :].astype(F32)
            scale = scale_of(x)
            da = acc[r, :].astype(BF16).astype(F32)
            dot = jnp.mean(da * x, -1, keepdims=True)
            by = scale * da - x * (scale * scale * scale * dot)
            dh = (dy_ref[r, :].astype(F32) + by.astype(BF16).astype(F32)).astype(BF16)
            a[r, :] = dh
            dyt[:, r] = dh.T
            return _
        lax.fori_loop(0, tokens // CHUNK, out, 0)
        for one in saved(0):
            one.start()
        normed.wait()

    @pl.when((j >= tiles) & (j < 2 * tiles))
    def _():
        hold(wd_ref, wd, 0, left, at_end)
        for one in saved(j - tiles):
            one.wait()
        for c in range(tokens // WIDE):
            r = pl.ds(c * WIDE, WIDE)
            d = nt(a[r, :], wd[...]).astype(BF16).astype(F32)
            activations(wide[r, 0:TILE], wide[r, TILE : 2 * TILE], d, act, dgate, dup, r)

        @pl.when(j < 2 * tiles - 1)
        def _():
            for one in saved(j - tiles + 1):
                one.start()

    @pl.when(j < 2 * tiles)
    def _():
        tile_gradients(exchange.g, lax.rem(j, SLOTS), at, dyt, dgate, dup, act)

    exchange.step(j)

    @pl.when(j == pl.num_programs(0) - 1)
    def _():
        me = lax.axis_index("dp")
        n = lax.axis_size("dp")
        all_squares[me] = exchange.squares[...]
        copies = [
            pltpu.make_async_remote_copy(
                src_ref=exchange.squares, dst_ref=all_squares.at[me], send_sem=sent.at[k], recv_sem=arrived.at[k],
                device_id={"dp": lax.rem(me + k, n)}, device_id_type=MESH,
            )
            for k in range(1, n)
        ]
        for one in copies:
            one.start()
        for one in copies:
            one.wait()
        mean = jnp.sum(all_squares[...]) / count
        factor_ref[...] = jnp.full(factor_ref.shape, jnp.minimum(1.0, 0.5 * lax.rsqrt(mean + 1e-30)), F32)


def whole(shape):
    return pl.BlockSpec(shape, lambda j: (0,) * len(shape), pipeline_mode=pl.Buffered(1))


def params():
    return pltpu.CompilerParams(dimension_semantics=("arbitrary",), vmem_limit_bytes=62 * 1024 * 1024)


def forward(x, w, layer):
    tokens, d = x.shape
    ff = w[0].shape[2]
    tiles = pl.cdiv(ff, TILE)
    col = pl.BlockSpec((1, d, TILE), lambda j: (layer, 0, j))
    row = pl.BlockSpec((1, TILE, d), lambda j: (layer, j, 0))
    saved = pl.BlockSpec((tokens, TILE), lambda j: (0, j))
    return pl.pallas_call(
        functools.partial(forward_kernel, tokens // CHUNK, ff - (tiles - 1) * TILE),
        grid=(tiles,),
        in_specs=[whole((tokens, d)), col, col, row],
        out_specs=[whole((tokens, d)), whole((d, tokens)), saved, saved],
        out_shape=[jax.ShapeDtypeStruct((tokens, d), BF16), jax.ShapeDtypeStruct((d, tokens), BF16)] + [jax.ShapeDtypeStruct((tokens, tiles * TILE), F32)] * 2,
        scratch_shapes=[pltpu.VMEM((tokens, d), BF16), pltpu.VMEM((tokens, d), F32), pltpu.VMEM((d, TILE), BF16), pltpu.VMEM((d, TILE), BF16), pltpu.VMEM((TILE, d), BF16)],
        compiler_params=params(),
        cost_estimate=pl.CostEstimate(flops=6 * tokens * d * ff, bytes_accessed=8 * tokens * ff, transcendentals=tokens * ff),
        name="forward",
    )(x, *w)


def backward(h, dy, at, gate, up, w, n, count):
    tokens, d = h.shape
    ff = w[0].shape[2]
    tiles = pl.cdiv(ff, TILE)
    width, depth = 3 * TILE, d // n

    def late(j):
        return jnp.where(j < tiles, 1, 0)

    def tile(j):
        return jnp.minimum(jnp.where(j < tiles, j, j - tiles), tiles - 1)

    col = pl.BlockSpec((1, d, TILE), lambda j: (1, 0, jnp.minimum(j, tiles - 1)))
    row = pl.BlockSpec((1, TILE, d), lambda j: (late(j), tile(j), 0))
    hbm = pl.BlockSpec(memory_space=pl.ANY)
    return pl.pallas_call(
        functools.partial(backward_kernel, tiles, ff - (tiles - 1) * TILE, count),
        grid=(2 * tiles + 5,),
        in_specs=[whole((tokens, d)), whole((tokens, d)), hbm, hbm, hbm, col, col, row],
        out_specs=[hbm, hbm, whole((8, 128))],
        out_shape=[
            jax.ShapeDtypeStruct((d, width * tiles), BF16),
            jax.ShapeDtypeStruct((depth, width * tiles), BF16),
            jax.ShapeDtypeStruct((8, 128), F32),
        ],
        scratch_shapes=[
            pltpu.VMEM((tokens, d), BF16),
            pltpu.VMEM((d, tokens), BF16),
            pltpu.VMEM((d, tokens), BF16),
            pltpu.VMEM((tokens, TILE), BF16),
            pltpu.VMEM((tokens, TILE), BF16),
            pltpu.VMEM((tokens, TILE), BF16),
            pltpu.VMEM((tokens, 2 * TILE), F32),
            pltpu.VMEM((d, TILE), BF16),
            pltpu.VMEM((d, TILE), BF16),
            pltpu.VMEM((TILE, d), BF16),
            pltpu.SemaphoreType.DMA((3,)),
            pltpu.VMEM((n, 8, 128), F32),
            pltpu.SemaphoreType.DMA((n,)),
            pltpu.SemaphoreType.DMA((n,)),
            pltpu.VMEM((SLOTS, d, width), BF16),
            pltpu.VMEM((HALF_SLOTS, d // 2, width), BF16),
            pltpu.VMEM((2, RING_SLOTS, depth, width // 2), BF16),
            pltpu.VMEM((2, RING_SLOTS, depth, width), BF16),
            pltpu.VMEM((2 * tiles, depth, width), BF16),
            pltpu.VMEM((8, 128), F32),
            pltpu.SemaphoreType.DMA((13, 2 * tiles)),
            pltpu.SemaphoreType.DMA((13, 2 * tiles)),
            pltpu.SemaphoreType.DMA((2 * tiles,)),
        ],
        compiler_params=pltpu.CompilerParams(
            dimension_semantics=("arbitrary",), vmem_limit_bytes=67_000_000, collective_id=0, has_side_effects=True
        ),
        cost_estimate=pl.CostEstimate(flops=24 * tokens * d * ff, bytes_accessed=8 * tokens * ff, transcendentals=2 * tokens * ff),
        name="backward",
    )(h, dy, at, gate, up, *w)


def adamw_kernel(fresh, order, factor_ref, g_ref, *refs):
    w_refs, m_refs, v_refs = refs[0:3], refs[3:6], refs[6:9]
    outs = refs[9:] if fresh else refs[18:]
    factor = factor_ref[0, 0]
    for i in range(3):
        part = g_ref[:, i * TILE : (i + 1) * TILE]
        if order is not None:
            depth = part.shape[0] // len(order)
            part = jnp.concatenate([part[p * depth : (p + 1) * depth] for p in order])
        g = part.astype(F32) * factor
        if i == 2:
            g = g.T
        m = 0.9 * m_refs[i][0] + 0.1 * g
        v = 0.95 * v_refs[i][0] + 0.05 * g * g
        w = w_refs[i][0].astype(F32)
        outs[i][0] = (w - 0.02 * (m * lax.rsqrt(v + 1e-8) + 0.1 * w)).astype(BF16)
        outs[3 + i][0] = m
        outs[6 + i][0] = v


def adamw(factor, g, w, m, v, layer, order=None, so_far=None):
    layers, d, ff = w[0].shape
    tiles = pl.cdiv(ff, TILE)
    col = pl.BlockSpec((1, d, TILE), lambda j: (layer, 0, j))
    row = pl.BlockSpec((1, TILE, d), lambda j: (layer, j, 0))
    nine = [col, col, row] * 3
    arrays = [*w, *m, *v]
    held = [] if so_far is None else list(so_far)
    return pl.pallas_call(
        functools.partial(adamw_kernel, so_far is None, order),
        grid=(tiles,),
        in_specs=[pl.BlockSpec(memory_space=pltpu.SMEM), pl.BlockSpec((d, 3 * TILE), lambda j: (0, j))] + nine + [pl.BlockSpec(memory_space=pl.ANY)] * len(held),
        out_specs=nine,
        out_shape=[jax.ShapeDtypeStruct(a.shape, a.dtype) for a in arrays],
        input_output_aliases={11 + i: i for i in range(len(held))},
        compiler_params=params(),
        cost_estimate=pl.CostEstimate(flops=60 * d * ff, bytes_accessed=66 * d * ff, transcendentals=3 * d * ff),
        name="adamw",
    )(factor, g, *arrays, *held)


def solution(mesh):
    n = mesh.shape["dp"]
    order = [chip * 2 + core for core in range(2) for chip in range(n // 2)]

    def step(x, dy, *arrays):
        w, m, v = (arrays[i : i + 3] for i in (0, 3, 6))
        x, dy = x[0], dy[0]
        h, at, gate, up = forward(x, w, 0)
        g1, s0, factor = backward(h, dy, at, gate, up, w, n, sum(a.size for a in w))
        g0 = lax.all_gather(s0, "dp", axis=0, tiled=True)
        new = adamw(factor, g1, w, m, v, 1)
        return tuple(adamw(factor, g0, w, m, v, 0, order, new))

    return jax.shard_map(
        step,
        mesh=mesh,
        in_specs=(P(("rep", "dp"), None, None),) * 2 + (P(None, None, None),) * 9,
        out_specs=(P("rep", None, None),) * 9,
        check_vma=False,
    )
```

time: 539 us -> 430 us (0.80)
  waiting for transfers between devices: 146 us -> 13.5 us
  Pallas kernels: 356 us -> 402 us
  blocking collectives: 14.3 us -> 0 us
  other arithmetic: 5.9 us -> 0 us
    reduce_scatter x2 -> x0, waiting for transfers between devices: 83.7 us -> none  [the longest x1 76.4 us: step(): s0 = lax.psum_scatter(g0, 'dp', scatter_dimension=0, tiled=True)]
    pallas_call x4 -> x3, Pallas kernels: 297 us -> 354 us  [the longest x1 242 us: backward(): pl.pallas_call(functools.partial(backward_kernel, tiles, ff - (tiles - 1)...]
    all_gather x2 -> x1, waiting for transfers between devices: 62.5 us -> 13.5 us  [step(): g0 = lax.all_gather(s0, 'dp', axis=0, tiled=True)]
    psum x1 -> x0, blocking collectives: 14.3 us -> none  [step(): squares = lax.psum(squares, 'dp')]
    pallas_call x1, Pallas kernels: 59.1 us -> 48.2 us  [forward(): pl.pallas_call(functools.partial(forward_kernel, tokens // CHUNK, ff - (t...]
    reduce_sum x2 -> x0, other arithmetic: 5.9 us -> none  [step(): squares = sum((jnp.sum(s.astype(F32) ** 2) for s in (s1, s0)))]
  transfers between devices with their start and end apart: 4 -> 1, of which waited for: 4 -> 1; matrix products, arithmetic and copies ran while one was open for 1% -> 0% of each run, Pallas kernels for 23% -> 13%
where the time goes in v2:
time: 430 us
  Pallas kernels  402 us (93%)
  between operations  14.1 us (3%)
  waiting for transfers between devices  13.5 us (3%)
    pallas_call x1, Pallas kernels, backward(): pl.pallas_call(functools.partial(backward_kernel, tiles, ff - (tiles - 1)...  242 us
    pallas_call x2, Pallas kernels, adamw(): pl.pallas_call(functools.partial(adamw_kernel, so_far is None, order), gr...  112 us
    pallas_call x1, Pallas kernels, forward(): pl.pallas_call(functools.partial(forward_kernel, tokens // CHUNK, ff - (t...  48.2 us
    all_gather x1, waiting for transfers between devices, step(): g0 = lax.all_gather(s0, 'dp', axis=0, tiled=True)  13.5 us
  transfers between devices with their start and end apart: 1, of which 1 were waited for; matrix products, arithmetic and copies ran while one was open for 0% of the time, Pallas kernels for 13%

profile of v2, /device:TPU:113, one launch (start us, length us, event | category | flops | bytes accessed | tf_op | source)
XLA Modules:
  0.0 429.9 jit_solution(2054838787659012301)
XLA Ops:
  7.2 0.1 all-gather.2.cloned.1.call-start
  7.3 48.2 %forward.1 = (bf16[2048,640]{1,0:T(8,128)(2,1)}, bf16[640,2048]{1,0:T(8,128)(2,1)}, f32[2048,3584]{1,0:T(8,128)}, f32[2048,3584]{1,0:T(8,128)}) custom-call(bf16[2048,640]{1,0:T(8,128)(2,1)} %bitcast.2, bf16[2,640,3456]{2,1,0:T(8,128)(2,1)} %refs_0_.3, bf16[2,640,3456]{2,1,0:T(8,128)(2,1)} %refs_1_.3, bf16[2,3456,640]{2,1,0:T(8,128)(2,1)} %refs_2_.3), custom_call_target="tpu_custom_call" | custom-call | flops 27179089920 | bytes 56623104 | tf_op jit(solution)/shard_map/forward/pallas_call | solution.py:410
  55.4 241.9 %backward.1 = (bf16[640,10752]{1,0:T(8,128)(2,1)}, bf16[80,10752]{1,0:T(8,128)(2,1)}, f32[8,128]{1,0:T(8,128)}) custom-call(bf16[2048,640]{1,0:T(8,128)(2,1)} %get-tuple-element.25.h_ref, bf16[2048,640]{1,0:T(8,128)(2,1)} %bitcast.3, bf16[640,2048]{1,0:T(8,128)(2,1)} %get-tuple-element.26.at_ref, f32[2048,3584]{1,0:T(8,128)} %get-tuple-element.27.gate_ref, ...), custom_call_target="tpu_custom_call" | custom-call | flops 108716359680 | bytes 56623104 | tf_op jit(solution)/shard_map/backward/pallas_call | solution.py:438
  297.4 0.1 all-gather.2.cloned.1.call-update
  297.4 56.0 %adamw.2 = (bf16[2,640,3456]{2,1,0:T(8,128)(2,1)}, bf16[2,640,3456]{2,1,0:T(8,128)(2,1)}, bf16[2,3456,640]{2,1,0:T(8,128)(2,1)}, f32[2,640,3456]{2,1,0:T(8,128)}...) custom-call(f32[8,128]{1,0:T(8,128)} %get-tuple-element.29.factor_re, ...), custom_call_target="tpu_custom_call" | custom-call | flops 132710400 | bytes 145981440 | tf_op jit(solution)/shard_map/adamw/pallas_call | solution.py:509
  353.4 13.5 %all-gather.2.cloned.1.call-done.g_ref = bf16[640,10752]{1,0:T(8,128)(2,1)} async-done(((bf16[80,10752]{1,0:T(8,128)(2,1)}), bf16[640,10752]{1,0:T(8,128)(2,1)}) %all-gather.2.cloned.1.call-update) | async-done | bytes 13762576 | tf_op jit(solution)/shard_map/all_gather | solution.py:531
  366.9 56.1 %adamw.3 = (bf16[2,640,3456]{2,1,0:T(8,128)(2,1)}, bf16[2,640,3456]{2,1,0:T(8,128)(2,1)}, bf16[2,3456,640]{2,1,0:T(8,128)(2,1)}, f32[2,640,3456]{2,1,0:T(8,128)}...) custom-call(f32[8,128]{1,0:T(8,128)} %get-tuple-element.29.factor_re, ...), custom_call_target="tpu_custom_call", output_to_operand_aliasing={{0}: (11, {}), {1}: (12, {}), {2}: (13, {}), {3}: (14, {}),... | custom-call | flops 132710400 | bytes 145981440 | tf_op jit(solution)/shard_map/adamw/pallas_call | solution.py:509
Async XLA Ops:
  7.2 359.7 %all-gather.2.cloned.1.call-start = ((), (), s32[]{:S(2)}) async-start(), calls=%async_computation | async-start | bytes 15482880 | tf_op jit(solution)/shard_map/all_gather | solution.py:531
Sparse Core Ops, SparseCore 0:
  297.6 69.2 all-gather.1

commit v3 on v2

--- a/solution.py
+++ b/solution.py
@@ -10,7 +10,7 @@
 TILE = 512
 CHUNK = 1024
 WIDE = 2048
-SLOTS, HALF_SLOTS, RING_SLOTS = 4, 6, 3
+SLOTS, HALF_SLOTS, RING_SLOTS = 4, 6, 4
 MESH = pl.DeviceIdType.MESH
 
 
@@ -177,16 +177,27 @@
         def _():
             what(t)
 
-    def step(self, j):
-        everyone, alone = (0, self.gathered), (self.gathered, self.tiles)
+    def early(self, j):
+        soon = self.gathered - 1
+        self.stage(j, 1, self.far_block, 0, self.tiles)
+        self.stage(j, 2, self.neighbours, soon, self.tiles)
+        self.stage(j, 2, self.own_block, 0, soon)
+        self.stage(j, 3, self.forward_far, 0, soon - 1)
+
+    def midway(self, j):
+        self.stage(j, 1, self.neighbours, 0, self.gathered - 1)
+
+    def late(self, j):
+        soon = self.gathered - 1
         self.stage(j, 0, lambda t: self.swap(t).start(), 0, self.tiles)
-        self.stage(j, 6, self.finish, *everyone)
-        self.stage(j, 5, self.forward_far, *everyone)
-        self.stage(j, 4, self.forward_near, *everyone)
-        self.stage(j, 4, lambda t: self.kept_alone(t).wait(), *alone)
-        self.stage(j, 3, self.own_block, 0, self.tiles)
-        self.stage(j, 2, self.neighbours, 0, self.tiles)
-        self.stage(j, 1, self.far_block, 0, self.tiles)
+        self.stage(j, 3, self.own_block, soon, self.tiles)
+        self.stage(j, 4, lambda t: self.kept_alone(t).wait(), self.gathered, self.tiles)
+        self.stage(j, 3, self.finish, 0, soon - 1)
+        self.stage(j, 2, self.forward_near, 0, soon - 1)
+        for t, lag in ((soon - 1, 3), (soon, 4)):
+            self.stage(j, lag, self.forward_near, t, t + 1)
+            self.stage(j, lag + 1, self.forward_far, t, t + 1)
+            self.stage(j, lag + 2, self.finish, t, t + 1)
 
     def far_block(self, t):
         self.swap(t).wait_recv()
@@ -327,7 +338,16 @@
             d = nt(dy_ref[r, :], wd[...]).astype(BF16).astype(F32)
             d_gate, d_up = activations(gate, up, d, act, dgate, dup, r)
             acc[r, :] += nt(d_gate, wg[...]) + nt(d_up, wu[...])
-            return _
+
+            @pl.when(c == 0)
+            def _():
+                exchange.early(j)
+
+            @pl.when(c == 1)
+            def _():
+                exchange.midway(j)
+
+            return 0
         lax.fori_loop(0, tokens // CHUNK, body, 0)
 
     @pl.when(j == tiles)
@@ -366,11 +386,15 @@
             for one in saved(j - tiles + 1):
                 one.start()
 
+    @pl.when(j >= tiles)
+    def _():
+        exchange.early(j)
+
     @pl.when(j < 2 * tiles)
     def _():
         tile_gradients(exchange.g, lax.rem(j, SLOTS), at, dyt, dgate, dup, act)
 
-    exchange.step(j)
+    exchange.late(j)
 
     @pl.when(j == pl.num_programs(0) - 1)
     def _():
@@ -437,7 +461,7 @@
     hbm = pl.BlockSpec(memory_space=pl.ANY)
     return pl.pallas_call(
         functools.partial(backward_kernel, tiles, ff - (tiles - 1) * TILE, count),
-        grid=(2 * tiles + 5,),
+        grid=(2 * tiles + 4,),
         in_specs=[whole((tokens, d)), whole((tokens, d)), hbm, hbm, hbm, col, col, row],
         out_specs=[hbm, hbm, whole((8, 128))],
         out_shape=[

time: 430 us -> 407 us (0.947)
  Pallas kernels: 402 us -> 380 us
    pallas_call x1, Pallas kernels: 242 us -> 219 us  [backward(): pl.pallas_call(functools.partial(backward_kernel, tiles, ff - (tiles - 1)...]
  transfers between devices with their start and end apart: 1 -> 1, of which waited for: 1 -> 1; matrix products, arithmetic and copies ran while one was open for 0% -> 0% of each run, Pallas kernels for 13% -> 14%
where the time goes in v3:
time: 407 us
  Pallas kernels  380 us (93%)
  between operations  14.1 us (3%)
  waiting for transfers between devices  13 us (3%)
    pallas_call x1, Pallas kernels, backward(): pl.pallas_call(functools.partial(backward_kernel, tiles, ff - (tiles - 1)...  219 us
    pallas_call x2, Pallas kernels, adamw(): pl.pallas_call(functools.partial(adamw_kernel, so_far is None, order), gr...  112 us
    pallas_call x1, Pallas kernels, forward(): pl.pallas_call(functools.partial(forward_kernel, tokens // CHUNK, ff - (t...  48.2 us
    all_gather x1, waiting for transfers between devices, step(): g0 = lax.all_gather(s0, 'dp', axis=0, tiled=True)  13 us
  transfers between devices with their start and end apart: 1, of which 1 were waited for; matrix products, arithmetic and copies ran while one was open for 0% of the time, Pallas kernels for 14%

profile of v3, /device:TPU:113, one launch (start us, length us, event | category | flops | bytes accessed | tf_op | source)
XLA Modules:
  0.0 406.9 jit_solution(8690974851488382435)
XLA Ops:
  7.2 0.1 all-gather.2.cloned.1.call-start
  7.3 48.2 %forward.1 = (bf16[2048,640]{1,0:T(8,128)(2,1)}, bf16[640,2048]{1,0:T(8,128)(2,1)}, f32[2048,3584]{1,0:T(8,128)}, f32[2048,3584]{1,0:T(8,128)}) custom-call(bf16[2048,640]{1,0:T(8,128)(2,1)} %bitcast.2, bf16[2,640,3456]{2,1,0:T(8,128)(2,1)} %refs_0_.3, bf16[2,640,3456]{2,1,0:T(8,128)(2,1)} %refs_1_.3, bf16[2,3456,640]{2,1,0:T(8,128)(2,1)} %refs_2_.3), custom_call_target="tpu_custom_call" | custom-call | flops 27179089920 | bytes 56623104 | tf_op jit(solution)/shard_map/forward/pallas_call | solution.py:434
  55.4 219.4 %backward.1 = (bf16[640,10752]{1,0:T(8,128)(2,1)}, bf16[80,10752]{1,0:T(8,128)(2,1)}, f32[8,128]{1,0:T(8,128)}) custom-call(bf16[2048,640]{1,0:T(8,128)(2,1)} %get-tuple-element.25.h_ref, bf16[2048,640]{1,0:T(8,128)(2,1)} %bitcast.3, bf16[640,2048]{1,0:T(8,128)(2,1)} %get-tuple-element.26.at_ref, f32[2048,3584]{1,0:T(8,128)} %get-tuple-element.27.gate_ref, ...), custom_call_target="tpu_custom_call" | custom-call | flops 108716359680 | bytes 56623104 | tf_op jit(solution)/shard_map/backward/pallas_call | solution.py:462
  274.8 0.1 all-gather.2.cloned.1.call-update
  274.9 56.0 %adamw.2 = (bf16[2,640,3456]{2,1,0:T(8,128)(2,1)}, bf16[2,640,3456]{2,1,0:T(8,128)(2,1)}, bf16[2,3456,640]{2,1,0:T(8,128)(2,1)}, f32[2,640,3456]{2,1,0:T(8,128)}...) custom-call(f32[8,128]{1,0:T(8,128)} %get-tuple-element.29.factor_re, ...), custom_call_target="tpu_custom_call" | custom-call | flops 132710400 | bytes 145981440 | tf_op jit(solution)/shard_map/adamw/pallas_call | solution.py:533
  330.9 13.0 %all-gather.2.cloned.1.call-done.g_ref = bf16[640,10752]{1,0:T(8,128)(2,1)} async-done(((bf16[80,10752]{1,0:T(8,128)(2,1)}), bf16[640,10752]{1,0:T(8,128)(2,1)}) %all-gather.2.cloned.1.call-update) | async-done | bytes 13762576 | tf_op jit(solution)/shard_map/all_gather | solution.py:555
  343.9 56.1 %adamw.3 = (bf16[2,640,3456]{2,1,0:T(8,128)(2,1)}, bf16[2,640,3456]{2,1,0:T(8,128)(2,1)}, bf16[2,3456,640]{2,1,0:T(8,128)(2,1)}, f32[2,640,3456]{2,1,0:T(8,128)}...) custom-call(f32[8,128]{1,0:T(8,128)} %get-tuple-element.29.factor_re, ...), custom_call_target="tpu_custom_call", output_to_operand_aliasing={{0}: (11, {}), {1}: (12, {}), {2}: (13, {}), {3}: (14, {}),... | custom-call | flops 132710400 | bytes 145981440 | tf_op jit(solution)/shard_map/adamw/pallas_call | solution.py:533
Async XLA Ops:
  7.2 336.7 %all-gather.2.cloned.1.call-start = ((), (), s32[]{:S(2)}) async-start(), calls=%async_computation | async-start | bytes 15482880 | tf_op jit(solution)/shard_map/all_gather | solution.py:555
Sparse Core Ops, SparseCore 0:
  275.0 68.7 all-gather.1

commit v4 on v3

--- a/solution.py
+++ b/solution.py
@@ -11,6 +11,7 @@
 CHUNK = 1024
 WIDE = 2048
 SLOTS, HALF_SLOTS, RING_SLOTS = 4, 6, 4
+ROWS = 8
 MESH = pl.DeviceIdType.MESH
 
 
@@ -106,6 +107,7 @@
         self.chips, self.chip, self.core, self.right, self.left, self.across = place()
         self.depth, self.width = own.shape[1], own.shape[2]
         self.mid = self.width // 2
+        self.split = gathered + own_ref[0].shape[1] // self.width
 
     def copy(self, kind, t, src, dst, chip=None, core=None):
         to = (self.chip if chip is None else chip) * 2 + (self.core if core is None else core)
@@ -167,8 +169,10 @@
     def kept(self, t):
         return pltpu.make_async_copy(self.own.at[t], self.region(self.chip, t), self.local.at[t])
 
-    def kept_alone(self, t):
-        return pltpu.make_async_copy(self.own.at[t], self.own_ref.at[:, self.cols(t - self.gathered)], self.local.at[t])
+    def kept_alone(self, t, part):
+        ref = self.own_ref[part]
+        start = self.gathered if part == 0 else self.split
+        return pltpu.make_async_copy(self.own.at[t], ref.at[:, self.cols(t - start)], self.local.at[t])
 
     def stage(self, j, lag, what, start, stop):
         t = j - lag
@@ -191,7 +195,8 @@
         soon = self.gathered - 1
         self.stage(j, 0, lambda t: self.swap(t).start(), 0, self.tiles)
         self.stage(j, 3, self.own_block, soon, self.tiles)
-        self.stage(j, 4, lambda t: self.kept_alone(t).wait(), self.gathered, self.tiles)
+        self.stage(j, 4, lambda t: self.kept_alone(t, 0).wait(), self.gathered, self.split)
+        self.stage(j, 4, lambda t: self.kept_alone(t, 1).wait(), self.split, self.tiles)
         self.stage(j, 3, self.finish, 0, soon - 1)
         self.stage(j, 2, self.forward_near, 0, soon - 1)
         for t, lag in ((soon - 1, 3), (soon, 4)):
@@ -233,9 +238,13 @@
             for one in self.spread(t):
                 one.start()
 
-        @pl.when(t >= self.gathered)
+        @pl.when((t >= self.gathered) & (t < self.split))
         def _():
-            self.kept_alone(t).start()
+            self.kept_alone(t, 0).start()
+
+        @pl.when(t >= self.split)
+        def _():
+            self.kept_alone(t, 1).start()
 
         for one in (self.swap(t), *self.first(t), *self.second(t)):
             one.wait_send()
@@ -293,12 +302,12 @@
     return d_gate, d_up
 
 
-def backward_kernel(tiles, left, count, h_ref, dy_ref, at_ref, gate_ref, up_ref, wg_ref, wu_ref, wd_ref, all_ref, own_ref, factor_ref,
+def backward_kernel(tiles, left, count, h_ref, dy_ref, at_ref, gate_ref, up_ref, wg_ref, wu_ref, wd_ref, all_ref, own_one_ref, own_two_ref, factor_ref,
                     a, at, dyt, act, dgate, dup, wide, wg, wu, wd, loaded, all_squares, sent, arrived, *comm):
     j = pl.program_id(0)
     d = h_ref.shape[1]
     tokens = h_ref.shape[0]
-    exchange = Exchange(2 * tiles, tiles, all_ref, own_ref, *comm)
+    exchange = Exchange(2 * tiles, tiles, all_ref, (own_one_ref, own_two_ref), *comm)
     at_end = (j == tiles - 1) | (j == 2 * tiles - 1)
     acc = wide.at[:, 0:d]
 
@@ -463,10 +472,11 @@
         functools.partial(backward_kernel, tiles, ff - (tiles - 1) * TILE, count),
         grid=(2 * tiles + 4,),
         in_specs=[whole((tokens, d)), whole((tokens, d)), hbm, hbm, hbm, col, col, row],
-        out_specs=[hbm, hbm, whole((8, 128))],
+        out_specs=[hbm, hbm, hbm, whole((8, 128))],
         out_shape=[
             jax.ShapeDtypeStruct((d, width * tiles), BF16),
-            jax.ShapeDtypeStruct((depth, width * tiles), BF16),
+            jax.ShapeDtypeStruct((depth, width * (tiles - 3)), BF16),
+            jax.ShapeDtypeStruct((depth, width * 3), BF16),
             jax.ShapeDtypeStruct((8, 128), F32),
         ],
         scratch_shapes=[
@@ -502,59 +512,79 @@
     )(h, dy, at, gate, up, *w)
 
 
-def adamw_kernel(fresh, order, factor_ref, g_ref, *refs):
-    w_refs, m_refs, v_refs = refs[0:3], refs[3:6], refs[6:9]
-    outs = refs[9:] if fresh else refs[18:]
+def adamw_kernel(fresh, cores, factor_ref, g_ref, *refs):
+    nine, outs = refs[:9], refs[9:] if fresh else refs[18:]
     factor = factor_ref[0, 0]
-    for i in range(3):
-        part = g_ref[:, i * TILE : (i + 1) * TILE]
-        if order is not None:
-            depth = part.shape[0] // len(order)
-            part = jnp.concatenate([part[p * depth : (p + 1) * depth] for p in order])
-        g = part.astype(F32) * factor
-        if i == 2:
-            g = g.T
-        m = 0.9 * m_refs[i][0] + 0.1 * g
-        v = 0.95 * v_refs[i][0] + 0.05 * g * g
-        w = w_refs[i][0].astype(F32)
-        outs[i][0] = (w - 0.02 * (m * lax.rsqrt(v + 1e-8) + 0.1 * w)).astype(BF16)
-        outs[3 + i][0] = m
-        outs[6 + i][0] = v
-
-
-def adamw(factor, g, w, m, v, layer, order=None, so_far=None):
+    n = ROWS if cores is None else cores[0] * cores[1]
+    depth = g_ref.shape[0] // n
+
+    def block(b):
+        return b if cores is None else b % cores[1] * cores[0] + b // cores[1]
+
+    def one(i, g, r):
+        m = 0.9 * nine[3 + i][0, r, :] + 0.1 * g
+        v = 0.95 * nine[6 + i][0, r, :] + 0.05 * g * g
+        w = nine[i][0, r, :].astype(F32)
+        outs[i][0, r, :] = (w - 0.02 * (m * lax.rsqrt(v + 1e-8) + 0.1 * w)).astype(BF16)
+        outs[3 + i][0, r, :] = m
+        outs[6 + i][0, r, :] = v
+
+    def along(b, _):
+        r = pl.ds(pl.multiple_of(b * depth, 16), depth)
+        source = pl.ds(pl.multiple_of(block(b) * depth, 16), depth)
+        for i in range(2):
+            one(i, g_ref[source, i * TILE : (i + 1) * TILE].astype(F32) * factor, r)
+        return 0
+    lax.fori_loop(0, n, along, 0)
+
+    def across(c, _):
+        r = pl.ds(pl.multiple_of(c * 128, 128), 128)
+        cols = pl.ds(pl.multiple_of(2 * TILE + c * 128, 128), 128)
+        if cores is None:
+            g = g_ref[:, cols]
+        else:
+            g = jnp.concatenate([g_ref[pl.ds(block(b) * depth, depth), cols] for b in range(n)])
+        one(2, (g.astype(F32) * factor).T, r)
+        return 0
+    lax.fori_loop(0, TILE // 128, across, 0)
+
+
+def adamw(factor, g, w, m, v, layer, first, last, cores=None, so_far=None):
     layers, d, ff = w[0].shape
-    tiles = pl.cdiv(ff, TILE)
-    col = pl.BlockSpec((1, d, TILE), lambda j: (layer, 0, j))
-    row = pl.BlockSpec((1, TILE, d), lambda j: (layer, j, 0))
+    count = last - first
+    col = pl.BlockSpec((1, d, TILE), lambda j: (layer, 0, j + first))
+    row = pl.BlockSpec((1, TILE, d), lambda j: (layer, j + first, 0))
     nine = [col, col, row] * 3
     arrays = [*w, *m, *v]
     held = [] if so_far is None else list(so_far)
     return pl.pallas_call(
-        functools.partial(adamw_kernel, so_far is None, order),
-        grid=(tiles,),
+        functools.partial(adamw_kernel, so_far is None, cores),
+        grid=(count,),
         in_specs=[pl.BlockSpec(memory_space=pltpu.SMEM), pl.BlockSpec((d, 3 * TILE), lambda j: (0, j))] + nine + [pl.BlockSpec(memory_space=pl.ANY)] * len(held),
         out_specs=nine,
         out_shape=[jax.ShapeDtypeStruct(a.shape, a.dtype) for a in arrays],
         input_output_aliases={11 + i: i for i in range(len(held))},
         compiler_params=params(),
-        cost_estimate=pl.CostEstimate(flops=60 * d * ff, bytes_accessed=66 * d * ff, transcendentals=3 * d * ff),
+        cost_estimate=pl.CostEstimate(flops=60 * d * TILE * count, bytes_accessed=66 * d * TILE * count, transcendentals=3 * d * TILE * count),
         name="adamw",
     )(factor, g, *arrays, *held)
 
 
 def solution(mesh):
     n = mesh.shape["dp"]
-    order = [chip * 2 + core for core in range(2) for chip in range(n // 2)]
 
     def step(x, dy, *arrays):
         w, m, v = (arrays[i : i + 3] for i in (0, 3, 6))
         x, dy = x[0], dy[0]
         h, at, gate, up = forward(x, w, 0)
-        g1, s0, factor = backward(h, dy, at, gate, up, w, n, sum(a.size for a in w))
-        g0 = lax.all_gather(s0, "dp", axis=0, tiled=True)
-        new = adamw(factor, g1, w, m, v, 1)
-        return tuple(adamw(factor, g0, w, m, v, 0, order, new))
+        g1, *blocks, factor = backward(h, dy, at, gate, up, w, n, sum(a.size for a in w))
+        tiles = pl.cdiv(w[0].shape[2], TILE)
+        parts = [(0, tiles - 3), (tiles - 3, tiles)]
+        pieces = [lax.all_gather(s0, "dp", axis=0, tiled=True) for s0 in blocks]
+        new = adamw(factor, g1, w, m, v, 1, 0, tiles)
+        for (first, last), g0 in zip(parts, pieces, strict=True):
+            new = adamw(factor, g0, w, m, v, 0, first, last, (2, n // 2), new)
+        return tuple(new)
 
     return jax.shard_map(
         step,

time: 407 us -> 386 us (0.948)
  waiting for transfers between devices: 13 us -> 1.89 us
  Pallas kernels: 380 us -> 369 us
    all_gather x1 -> x2, waiting for transfers between devices: 13 us -> 1.11 us  [step(): pieces = [lax.all_gather(s0, 'dp', axis=0, tiled=True) for s0 in blocks]]
    pallas_call x2 -> x3, Pallas kernels: 112 us -> 102 us  [adamw(): pl.pallas_call(functools.partial(adamw_kernel, so_far is None, cores), gr...]
  transfers between devices with their start and end apart: 1 -> 2, of which waited for: 1 -> 1; matrix products, arithmetic and copies ran while one was open for 0% -> 0% of each run, Pallas kernels for 14% -> 20%
where the time goes in v4:
time: 386 us; the launch traced here: 385 us
  Pallas kernels  369 us (96%)
  between operations  14.1 us (4%)
    pallas_call x1, Pallas kernels, backward(): pl.pallas_call(functools.partial(backward_kernel, tiles, ff - (tiles - 1)...  220 us
    pallas_call x3, Pallas kernels, adamw(): pl.pallas_call(functools.partial(adamw_kernel, so_far is None, cores), gr...  102 us
    pallas_call x1, Pallas kernels, forward(): pl.pallas_call(functools.partial(forward_kernel, tokens // CHUNK, ff - (t...  48.1 us
  transfers between devices with their start and end apart: 2, of which 1 were waited for; matrix products, arithmetic and copies ran while one was open for 0% of the time, Pallas kernels for 20%

profile of v4, /device:TPU:113, one launch (start us, length us, event | category | flops | bytes accessed | tf_op | source)
XLA Modules:
  0.0 385.5 jit_solution(6264000496306457359)
XLA Ops:
  7.2 0.1 all-gather.5.cloned.1.call-start
  7.3 48.1 %forward.1 = (bf16[2048,640]{1,0:T(8,128)(2,1)}, bf16[640,2048]{1,0:T(8,128)(2,1)}, f32[2048,3584]{1,0:T(8,128)}, f32[2048,3584]{1,0:T(8,128)}) custom-call(bf16[2048,640]{1,0:T(8,128)(2,1)} %bitcast.2, bf16[2,640,3456]{2,1,0:T(8,128)(2,1)} %refs_0_.5, bf16[2,640,3456]{2,1,0:T(8,128)(2,1)} %refs_1_.5, bf16[2,3456,640]{2,1,0:T(8,128)(2,1)} %refs_2_.5), custom_call_target="tpu_custom_call" | custom-call | flops 27179089920 | bytes 56623104 | tf_op jit(solution)/shard_map/forward/pallas_call | solution.py:443
  55.3 219.5 %backward.1 = (bf16[640,10752]{1,0:T(8,128)(2,1)}, bf16[80,6144]{1,0:T(8,128)(2,1)}, bf16[80,4608]{1,0:T(8,128)(2,1)}, f32[8,128]{1,0:T(8,128)}) custom-call(bf16[2048,640]{1,0:T(8,128)(2,1)} %get-tuple-element.35.h_ref, bf16[2048,640]{1,0:T(8,128)(2,1)} %bitcast.3, bf16[640,2048]{1,0:T(8,128)(2,1)} %get-tuple-element.36.at_ref, ...), custom_call_target="tpu_custom_call" | custom-call | flops 108716359680 | bytes 56623104 | tf_op jit(solution)/shard_map/backward/pallas_call | solution.py:471
  274.8 0.1 all-gather.5.cloned.1.call-update
  274.9 0.1 all-gather.3.cloned.1.call-start
  275.0 0.7 all-gather.3.cloned.1.call-update
  275.7 50.7 %adamw.3 = (bf16[2,640,3456]{2,1,0:T(8,128)(2,1)}, bf16[2,640,3456]{2,1,0:T(8,128)(2,1)}, bf16[2,3456,640]{2,1,0:T(8,128)(2,1)}, f32[2,640,3456]{2,1,0:T(8,128)}...) custom-call(f32[8,128]{1,0:T(8,128)} %get-tuple-element.39.factor_re, ...), custom_call_target="tpu_custom_call" | custom-call | flops 137625600 | bytes 151388160 | tf_op jit(solution)/shard_map/adamw/pallas_call | solution.py:560
  326.5 0.0 all-gather.5.cloned.1.call-done.g_ref
  326.5 27.9 %adamw.4 = (bf16[2,640,3456]{2,1,0:T(8,128)(2,1)}, bf16[2,640,3456]{2,1,0:T(8,128)(2,1)}, bf16[2,3456,640]{2,1,0:T(8,128)(2,1)}, f32[2,640,3456]{2,1,0:T(8,128)}...) custom-call(f32[8,128]{1,0:T(8,128)} %get-tuple-element.39.factor_re, ...), custom_call_target="tpu_custom_call", output_to_operand_aliasing={{0}: (11, {}), {1}: (12, {}), {2}: (13, {}), {3}: (14, {}),... | custom-call | flops 78643200 | bytes 86507520 | tf_op jit(solution)/shard_map/adamw/pallas_call | solution.py:560
  354.3 1.1 all-gather.3.cloned.1.call-done.g_ref
  355.4 23.1 %adamw.5 = (bf16[2,640,3456]{2,1,0:T(8,128)(2,1)}, bf16[2,640,3456]{2,1,0:T(8,128)(2,1)}, bf16[2,3456,640]{2,1,0:T(8,128)(2,1)}, f32[2,640,3456]{2,1,0:T(8,128)}...) custom-call(f32[8,128]{1,0:T(8,128)} %get-tuple-element.39.factor_re, ...), custom_call_target="tpu_custom_call", output_to_operand_aliasing={{0}: (11, {}), {1}: (12, {}), {2}: (13, {}), {3}: (14, {}),... | custom-call | flops 58982400 | bytes 64880640 | tf_op jit(solution)/shard_map/adamw/pallas_call | solution.py:560
Async XLA Ops:
  7.2 319.3 %all-gather.5.cloned.1.call-start = ((), (), s32[]{:S(2)}) async-start(), calls=%async_computation.1 | async-start | bytes 8847360 | tf_op jit(solution)/shard_map/all_gather | solution.py:583
  274.9 80.5 %all-gather.3.cloned.1.call-start = ((), (), s32[]{:S(2)}) async-start(), calls=%async_computation | async-start | bytes 6635520 | tf_op jit(solution)/shard_map/all_gather | solution.py:583
Sparse Core Ops, SparseCore 0:
  275.0 43.7 all-gather.4
  320.4 35.0 all-gather.2
